TPU v7x, 1024 devices: a whole 4x8x16 slice. The times are simulated.
1024 devices in a mesh: section: 16 (over y, core), dp: 4 (over z_lo), tensor: 16 (over x, z_hi).
Axes of the slice: x: 4, y: 8, z: 16 (z_hi: 4, z_lo: 4; z = z_hi * 4 + z_lo), core: 2. Of those that a mesh axis runs over, the one named last changes fastest.
Arguments:
- shadow_weight_copy: bfloat16 [16, 4096, 4096], P('section', None, 'tensor'), may hold values from -6 to 6
- newest_weight_version: bfloat16 [16, 4096, 4096], P('section', 'dp', 'tensor'), may hold values from -6 to 6
- momentum: bfloat16 [16, 4096, 4096], P('section', 'dp', 'tensor'), may hold values from -3 to 3
- pending_section_input: bfloat16 [4, 16, 64, 4096], P('dp', 'section', None, 'tensor'), may hold values from -16 to 16
- incoming_micro_input: bfloat16 [4, 3, 64, 4096], P('dp', None, None, 'tensor'), may hold values from -16 to 16
- pending_output_gradient: bfloat16 [4, 16, 64, 4096], P('dp', 'section', None, 'tensor'), may hold values from -16 to 16
- loss_gradient_rows: bfloat16 [4, 3, 64, 4096], P('dp', None, None, 'tensor'), may hold values from -16 to 16
- stashed: bfloat16 [4, 16, 4, 64, 4096], P('dp', 'section', None, None, 'tensor'), may hold values from -16 to 16
Outputs:
- forward_out: bfloat16 [4, 16, 4, 64, 4096], P('dp', 'section', None, None, 'tensor')
- backward_out: bfloat16 [4, 16, 4, 64, 4096], P('dp', 'section', None, None, 'tensor')
- w_next: bfloat16 [16, 4096, 4096], P('section', 'dp', 'tensor')
- m_next: bfloat16 [16, 4096, 4096], P('section', 'dp', 'tensor')
All inputs are finite; a program needn't handle non-finite values.
Results may differ from a plain program's by a relative error of at most 0.025.
Values may be sent and summed in bfloat16 or wider, within the bound.
A program may use at most 64 MiB of HBM per device.

v0:
```python
import math

import jax
import jax.numpy as jnp
from jax import lax
from jax.sharding import PartitionSpec as P

EPSILON = 1e-06
MOMENTUM_RATE = 0.9
LEARNING_RATE = 0.05


def shifted(block, axis, distance):
    devices = range(lax.axis_size(axis))
    route = [(i - distance, i) for i in devices if i - distance in devices]
    return lax.ppermute(block, axis, route)


def side_by_side(arrays, axis, dim, along):
    widths = [a.shape[along] for a in arrays]
    both = jnp.concatenate(arrays, axis=along)
    out = lax.all_gather(both, axis, axis=dim, tiled=True)
    return tuple(jnp.split(out, [sum(widths[:k]) for k in range(1, len(widths))], axis=along))


def cut_along(array, dim, length):
    before, after = (array.shape[:dim], array.shape[dim + 1 :])
    return jnp.moveaxis(array.reshape(*before, length, -1, *after), dim, 0)


def sent_and_summed(array, axis, dim):
    length = lax.axis_size(axis)
    parts = lax.all_to_all(cut_along(array, dim, length), axis, 0, 0, tiled=True)
    return jnp.sum(parts.astype(jnp.float32), axis=0)


def from_everyone(array, axis):
    length = lax.axis_size(axis)
    return lax.all_to_all(
        jnp.broadcast_to(array[None], (length, *array.shape)), axis, 0, 0, tiled=True
    )


def over_copies(array, axis):
    return from_everyone(array, axis).sum(axis=0)


def normalized(values):
    factor = lax.rsqrt(jnp.mean(values * values, axis=-1, keepdims=True) + EPSILON)
    return (values * factor, factor)


def body(
    shadow_weight_copy,
    newest_weight_version,
    momentum,
    pending_section_input,
    incoming_micro_input,
    pending_output_gradient,
    loss_gradient_rows,
    stashed,
):
    weight = shadow_weight_copy[0]
    extent = weight.shape[0]
    own_cols = weight.shape[1]
    root_width = math.sqrt(extent)
    tick_count = stashed.shape[2]
    section_count = lax.axis_size("section")
    is_first = lax.axis_index("section") == 0
    is_last = lax.axis_index("section") == section_count - 1
    col_start = lax.axis_index("tensor") * own_cols
    current_input = pending_section_input[0, 0]
    current_gradient = pending_output_gradient[0, 0]
    forward_list = []
    backward_list = []
    kept_list = []
    grad_list = []
    for tick_index in range(tick_count):
        if tick_index > 0:
            from_below = shifted(forward_list[-1], "section", 1)
            current_input = jnp.where(is_first, incoming_micro_input[0, tick_index - 1], from_below)
            from_above = shifted(backward_list[-1], "section", -1)
            current_gradient = jnp.where(is_last, loss_gradient_rows[0, tick_index - 1], from_above)
        whole_x, whole_kept = side_by_side(
            (current_input, stashed[0, 0, tick_index]), "tensor", 1, 0
        )
        x_hat, unused = normalized(whole_x.astype(jnp.float32))
        branch = (
            jnp.dot(x_hat.astype(jnp.bfloat16), weight, preferred_element_type=jnp.float32)
            / root_width
        )
        forward_list.append((current_input.astype(jnp.float32) + branch).astype(jnp.bfloat16))
        kept_hat, kept_factor = normalized(whole_kept.astype(jnp.float32))
        partial_value = (
            lax.dot_general(
                current_gradient,
                weight,
                (((1,), (1,)), ((), ())),
                preferred_element_type=jnp.float32,
            )
            / root_width
        ).astype(jnp.bfloat16)
        own_hat = lax.dynamic_slice_in_dim(kept_hat, col_start, own_cols, 1)
        own_grad = sent_and_summed(partial_value, "tensor", 1)
        inner_dot = (
            over_copies(jnp.sum(own_grad * own_hat, axis=-1, keepdims=True), "tensor") / extent
        )
        input_grad = (
            current_gradient.astype(jnp.float32) + (own_grad - own_hat * inner_dot) * kept_factor
        )
        backward_list.append(input_grad.astype(jnp.bfloat16))
        kept_list.append(kept_hat.astype(jnp.bfloat16))
        grad_list.append(current_gradient)
    kept_rows = jnp.concatenate(kept_list, axis=0)
    grad_rows = jnp.concatenate(grad_list, axis=0)
    replica_term = (
        lax.dot_general(
            kept_rows, grad_rows, (((0,), (0,)), ((), ())), preferred_element_type=jnp.float32
        )
        / root_width
    ).astype(jnp.bfloat16)
    summed = sent_and_summed(replica_term, "dp", 0)
    velocity = MOMENTUM_RATE * momentum[0].astype(jnp.float32) + summed
    w_next = (newest_weight_version[0].astype(jnp.float32) - LEARNING_RATE * velocity).astype(
        jnp.bfloat16
    )[None]
    m_next = velocity.astype(jnp.bfloat16)[None]
    forward_out = jnp.stack(forward_list, axis=0)[None, None]
    backward_out = jnp.stack(backward_list, axis=0)[None, None]
    return (forward_out, backward_out, w_next, m_next)


def solution(mesh):
    return jax.shard_map(
        body,
        mesh=mesh,
        in_specs=(
            P("section", None, "tensor"),
            P("section", "dp", "tensor"),
            P("section", "dp", "tensor"),
            P("dp", "section", None, "tensor"),
            P("dp", None, None, "tensor"),
            P("dp", "section", None, "tensor"),
            P("dp", None, None, "tensor"),
            P("dp", "section", None, None, "tensor"),
        ),
        out_specs=(
            P("dp", "section", None, None, "tensor"),
            P("dp", "section", None, None, "tensor"),
            P("section", "dp", "tensor"),
            P("section", "dp", "tensor"),
        ),
        check_vma=False,
    )
```

profile of v0, /device:TPU:1, one launch (start us, length us, event | category | flops | bytes accessed | tf_op | source)
XLA Modules:
  0.0 528.0 jit_solution(17367479834957022335)
XLA Ops:
  7.2 1.0 slice_bitcast_fusion
  8.2 1.4 pad_maximum_fusion
  9.6 1.5 fusion.1
  11.1 0.8 copy.27
  12.0 21.9 %all-to-all-start = ((bf16[16,64,256]{2,1,0:T(8,128)(2,1)}), bf16[16,64,256]{2,1,0:T(8,128)(2,1)}, u32[]{:S(2)}, u32[]{:S(2)}) async-start(bf16[16,64,256]{2,1,0:T(8,128)(2,1)} %bitcast.112), calls=%async_computation | async-start | bytes 1048576 | tf_op jit(solution)/shard_map/all_to_all | solution.py:33
  33.9 89.9 %all-gather.5.cloned.1.call-done = bf16[128,4096]{1,0:T(8,128)(2,1)} async-done(((bf16[128,256]{1,0:T(8,128)(2,1)}), bf16[128,4096]{1,0:T(8,128)(2,1)}) %all-gather.5.cloned.1.call-update) | async-done | bytes 1048592 | tf_op jit(solution)/shard_map/all_gather | solution.py:22
  123.8 1.6 fusion.50
  125.4 1.6 fusion.39
  127.0 2.8 collective-permute-start
  129.8 1.1 convert_reduce_fusion.4
  130.9 0.8 bitcast_select_fusion.5
  132.4 1.0 fusion.90
  133.4 1.0 copy-done.5
  134.5 17.5 %all_to_all.45 = f32[16,64,1]{1,2,0:T(1,128)S(1)} all-to-all(f32[16,64,1]{1,2,0:T(1,128)S(1)} %broadcast_in_dim.13), channel_id=1, replica_groups=mesh['section'=16,'dp'=4,'tensor'=16] {'tensor'}, dimensions={0} | all-to-all | bytes 8192 | tf_op jit(solution)/shard_map/all_to_all | solution.py:39
  152.1 0.9 add_convert_fusion.3
  153.0 2.4 collective-permute-start.3
  155.4 4.7 collective-permute-done.3
  160.1 0.8 bitcast_select_fusion.2
  161.6 0.8 copy.26
  162.5 4.2 all-to-all-start.2
  166.8 65.7 %all-gather.7.cloned.1.call-done = bf16[128,4096]{1,0:T(8,128)(2,1)} async-done(((bf16[128,256]{1,0:T(8,128)(2,1)}), bf16[128,4096]{1,0:T(8,128)(2,1)}) %all-gather.7.cloned.1.call-update) | async-done | bytes 1048592 | tf_op jit(solution)/shard_map/all_gather | solution.py:22
  232.4 1.6 fusion.51
  234.0 1.6 add_convert_fusion.6
  235.6 2.8 collective-permute-start.1
  238.4 1.0 collective-permute-done.1
  239.4 0.8 bitcast_select_fusion.4
  240.8 1.4 fusion.91
  242.2 1.1 convert_reduce_fusion.3
  243.3 1.0 multiply_reduce_fusion.2
  244.3 17.5 %all_to_all.46 = f32[16,64,1]{1,2,0:T(1,128)S(1)} all-to-all(f32[16,64,1]{1,2,0:T(1,128)S(1)} %broadcast_in_dim.14), channel_id=1, replica_groups=mesh['section'=16,'dp'=4,'tensor'=16] {'tensor'}, dimensions={0} | all-to-all | bytes 8192 | tf_op jit(solution)/shard_map/all_to_all | solution.py:39
  261.9 0.9 add_convert_fusion.2
  262.8 2.2 collective-permute-start.4
  265.0 5.0 collective-permute-done.4
  270.1 0.8 bitcast_select_fusion.1
  271.6 0.8 copy.25
  272.4 4.2 all-to-all-start.4
  276.7 57.6 %all-gather.9.cloned.1.call-done = bf16[128,4096]{1,0:T(8,128)(2,1)} async-done(((bf16[128,256]{1,0:T(8,128)(2,1)}), bf16[128,4096]{1,0:T(8,128)(2,1)}) %all-gather.9.cloned.1.call-update) | async-done | bytes 1048592 | tf_op jit(solution)/shard_map/all_gather | solution.py:22
  334.3 1.6 fusion.52
  335.9 1.6 add_convert_fusion.5
  337.5 3.7 collective-permute-start.2
  341.3 1.0 collective-permute-done.2
  342.2 0.8 bitcast_select_fusion.3
  343.7 1.4 fusion.92
  345.0 1.1 convert_reduce_fusion.2
  346.2 1.0 multiply_reduce_fusion.1
  347.1 17.5 %all_to_all.47 = f32[16,64,1]{1,2,0:T(1,128)S(1)} all-to-all(f32[16,64,1]{1,2,0:T(1,128)S(1)} %broadcast_in_dim.15), channel_id=1, replica_groups=mesh['section'=16,'dp'=4,'tensor'=16] {'tensor'}, dimensions={0} | all-to-all | bytes 8192 | tf_op jit(solution)/shard_map/all_to_all | solution.py:39
  364.7 0.9 add_convert_fusion.1
  365.6 3.5 collective-permute-start.5
  369.1 3.6 collective-permute-done.5
  372.7 0.8 bitcast_select_fusion
  374.2 0.8 copy.24
  375.1 3.6 all-to-all-start.6
  378.7 57.0 %all-gather.11.cloned.1.call-done = bf16[128,4096]{1,0:T(8,128)(2,1)} async-done(((bf16[128,256]{1,0:T(8,128)(2,1)}), bf16[128,4096]{1,0:T(8,128)(2,1)}) %all-gather.11.cloned.1.call-update) | async-done | bytes 1048592 | tf_op jit(solution)/shard_map/all_gather | solution.py:22
  435.7 1.5 fusion.53
  437.2 2.5 fusion.93
  439.8 1.0 multiply_reduce_fusion
  441.4 6.6 %all-to-all-start.7 = ((f32[16,64,1]{1,2,0:T(1,128)}), f32[16,64,1]{1,2,0:T(1,128)S(1)}, u32[]{:S(2)}, u32[]{:S(2)}) async-start(f32[16,64,1]{1,2,0:T(1,128)} %broadcast_in_dim.16), calls=%async_computation.7 | async-start | bytes 16384 | tf_op jit(solution)/shard_map/all_to_all | solution.py:39
  448.0 3.5 fusion
  451.5 10.1 %all-to-all-done.7 = f32[16,64,1]{1,2,0:T(1,128)S(1)} async-done(((f32[16,64,1]{1,2,0:T(1,128)}), f32[16,64,1]{1,2,0:T(1,128)S(1)}, u32[]{:S(2)}, u32[]{:S(2)}) %all-to-all-start.7) | async-done | bytes 4128 | tf_op jit(solution)/shard_map/all_to_all | solution.py:39
  461.5 8.7 %all-to-all-start.8 = ((bf16[4,1024,256]{2,1,0:T(8,128)(2,1)}), bf16[4,1024,256]{2,1,0:T(8,128)(2,1)}, u32[]{:S(2)}, u32[]{:S(2)}) async-start(bf16[4,1024,256]{2,1,0:T(8,128)(2,1)} %bitcast.113), calls=%async_computation.8 | async-start | bytes 4194304 | tf_op jit(solution)/shard_map/all_to_all | solution.py:33
  471.5 0.9 fusion.75
  473.2 45.0 %all-to-all-done.8 = bf16[4,1024,256]{2,1,0:T(8,128)(2,1)} async-done(((bf16[4,1024,256]{2,1,0:T(8,128)(2,1)}), bf16[4,1024,256]{2,1,0:T(8,128)(2,1)}, u32[]{:S(2)}, u32[]{:S(2)}) %all-to-all-start.8) | async-done | bytes 2097184 | tf_op jit(solution)/shard_map/all_to_all | solution.py:33
  518.1 2.0 convert_reduce_fusion
  520.2 1.3 fusion.54
  (65 shorter events, 7.4 us)
Async XLA Ops:
  7.2 2.4 copy-start
  7.2 116.6 %all-gather.5.cloned.1.call-start = ((), (), s32[]{:S(2)}) async-start(), calls=%async_computation.9 | async-start | bytes 1114112 | tf_op jit(solution)/shard_map/all_gather | solution.py:22
  11.1 114.3 %copy-start.9 = (bf16[1,1,64,256]{3,2,1,0:T(8,128)(2,1)S(1)}, bf16[1,1,64,256]{3,2,1,0:T(8,128)(2,1)}, u32[]{:S(2)}) copy-start(bf16[1,1,64,256]{3,2,1,0:T(8,128)(2,1)} %param.11) | copy-start | bytes 98308
  12.0 117.8 %all-to-all-start = ((bf16[16,64,256]{2,1,0:T(8,128)(2,1)}), bf16[16,64,256]{2,1,0:T(8,128)(2,1)}, u32[]{:S(2)}, u32[]{:S(2)}) async-start(bf16[16,64,256]{2,1,0:T(8,128)(2,1)} %bitcast.112), calls=%async_computation | async-start | bytes 1048576 | tf_op jit(solution)/shard_map/all_to_all | solution.py:33
  33.9 198.6 %all-gather.7.cloned.1.call-start = ((), (), s32[]{:S(2)}) async-start(), calls=%async_computation.10 | async-start | bytes 1114112 | tf_op jit(solution)/shard_map/all_gather | solution.py:22
  123.8 8.6 %copy-start.3 = (bf16[128,4096]{1,0:T(8,128)(2,1)S(1)}, bf16[128,4096]{1,0:T(8,128)(2,1)}, u32[]{:S(2)}) copy-start(bf16[128,4096]{1,0:T(8,128)(2,1)} %all-gather.5.cloned.1.call-done) | copy-start | bytes 3145732
  127.0 25.1 %copy-start.10 = (bf16[1,1,64,256]{3,2,1,0:T(8,128)(2,1)S(1)}, bf16[1,1,64,256]{3,2,1,0:T(8,128)(2,1)}, u32[]{:S(2)}) copy-start(bf16[1,1,64,256]{3,2,1,0:T(8,128)(2,1)} %param.13) | copy-start | bytes 98308
  127.0 3.9 collective-permute-start
  133.4 1.0 copy-start.5
  153.0 7.1 %collective-permute-start.3 = (bf16[64,256]{1,0:T(8,128)(2,1)S(1)}, bf16[64,256]{1,0:T(8,128)(2,1)S(1)}, u32[]{:S(2)}, u32[]{:S(2)}) collective-permute-start(bf16[64,256]{1,0:T(8,128)(2,1)S(1)} %add_convert_fusion.3), channel_id=1, source_target_pairs={{64,0},{128,64},{192,128},{256,192},{320,256},{384,320},{448,384},... | collective-permute-start | bytes 98312 | tf_op jit(solution)/shard_map/ppermute | solution.py:16
  162.5 79.7 %all-to-all-start.2 = ((bf16[16,64,256]{2,1,0:T(8,128)(2,1)}), bf16[16,64,256]{2,1,0:T(8,128)(2,1)}, u32[]{:S(2)}, u32[]{:S(2)}) async-start(bf16[16,64,256]{2,1,0:T(8,128)(2,1)} %bitcast.110), calls=%async_computation.2 | async-start | bytes 1048576 | tf_op jit(solution)/shard_map/all_to_all | solution.py:33
  166.7 167.6 %all-gather.9.cloned.1.call-start = ((), (), s32[]{:S(2)}) async-start(), calls=%async_computation.11 | async-start | bytes 1114112 | tf_op jit(solution)/shard_map/all_gather | solution.py:22
  232.4 8.4 %copy-start.4 = (bf16[128,4096]{1,0:T(8,128)(2,1)S(1)}, bf16[128,4096]{1,0:T(8,128)(2,1)}, u32[]{:S(2)}) copy-start(bf16[128,4096]{1,0:T(8,128)(2,1)} %all-gather.7.cloned.1.call-done) | copy-start | bytes 3145732
  235.6 3.8 collective-permute-start.1
  262.8 7.2 %collective-permute-start.4 = (bf16[64,256]{1,0:T(8,128)(2,1)S(1)}, bf16[64,256]{1,0:T(8,128)(2,1)S(1)}, u32[]{:S(2)}, u32[]{:S(2)}) collective-permute-start(bf16[64,256]{1,0:T(8,128)(2,1)S(1)} %add_convert_fusion.2), channel_id=1, source_target_pairs={{64,0},{128,64},{192,128},{256,192},{320,256},{384,320},{448,384},... | collective-permute-start | bytes 98312 | tf_op jit(solution)/shard_map/ppermute | solution.py:16
  272.4 72.6 %all-to-all-start.4 = ((bf16[16,64,256]{2,1,0:T(8,128)(2,1)}), bf16[16,64,256]{2,1,0:T(8,128)(2,1)}, u32[]{:S(2)}, u32[]{:S(2)}) async-start(bf16[16,64,256]{2,1,0:T(8,128)(2,1)} %bitcast.108), calls=%async_computation.4 | async-start | bytes 1048576 | tf_op jit(solution)/shard_map/all_to_all | solution.py:33
  276.7 159.0 %all-gather.11.cloned.1.call-start = ((), (), s32[]{:S(2)}) async-start(), calls=%async_computation.12 | async-start | bytes 1114112 | tf_op jit(solution)/shard_map/all_gather | solution.py:22
  334.3 9.4 %copy-start.2 = (bf16[128,4096]{1,0:T(8,128)(2,1)S(1)}, bf16[128,4096]{1,0:T(8,128)(2,1)}, u32[]{:S(2)}) copy-start(bf16[128,4096]{1,0:T(8,128)(2,1)} %all-gather.9.cloned.1.call-done) | copy-start | bytes 3145732
  337.5 4.7 collective-permute-start.2
  365.6 7.1 %collective-permute-start.5 = (bf16[64,256]{1,0:T(8,128)(2,1)S(1)}, bf16[64,256]{1,0:T(8,128)(2,1)S(1)}, u32[]{:S(2)}, u32[]{:S(2)}) collective-permute-start(bf16[64,256]{1,0:T(8,128)(2,1)S(1)} %add_convert_fusion.1), channel_id=1, source_target_pairs={{64,0},{128,64},{192,128},{256,192},{320,256},{384,320},{448,384},... | collective-permute-start | bytes 98312 | tf_op jit(solution)/shard_map/ppermute | solution.py:16
  375.1 64.6 %all-to-all-start.6 = ((bf16[16,64,256]{2,1,0:T(8,128)(2,1)}), bf16[16,64,256]{2,1,0:T(8,128)(2,1)S(1)}, u32[]{:S(2)}, u32[]{:S(2)}) async-start(bf16[16,64,256]{2,1,0:T(8,128)(2,1)} %bitcast.106), calls=%async_computation.6 | async-start | bytes 1048576 | tf_op jit(solution)/shard_map/all_to_all | solution.py:33
  378.7 69.3 %copy-start.6 = (bf16[64,4096]{1,0:T(8,128)(2,1)S(1)}, bf16[64,4096]{1,0:T(8,128)(2,1)}, u32[]{:S(2)}) copy-start(bf16[64,4096]{1,0:T(8,128)(2,1)} %get-tuple-element.14) | copy-start | bytes 1572868
  441.4 20.2 %all-to-all-start.7 = ((f32[16,64,1]{1,2,0:T(1,128)}), f32[16,64,1]{1,2,0:T(1,128)S(1)}, u32[]{:S(2)}, u32[]{:S(2)}) async-start(f32[16,64,1]{1,2,0:T(1,128)} %broadcast_in_dim.16), calls=%async_computation.7 | async-start | bytes 16384 | tf_op jit(solution)/shard_map/all_to_all | solution.py:39
  461.5 8.7 %copy-start.1 = (bf16[128,4096]{1,0:T(8,128)(2,1)S(1)}, bf16[128,4096]{1,0:T(8,128)(2,1)}, u32[]{:S(2)}) copy-start(bf16[128,4096]{1,0:T(8,128)(2,1)} %all-gather.11.cloned.1.call-done) | copy-start | bytes 3145732
  461.5 56.6 %all-to-all-start.8 = ((bf16[4,1024,256]{2,1,0:T(8,128)(2,1)}), bf16[4,1024,256]{2,1,0:T(8,128)(2,1)}, u32[]{:S(2)}, u32[]{:S(2)}) async-start(bf16[4,1024,256]{2,1,0:T(8,128)(2,1)} %bitcast.113), calls=%async_computation.8 | async-start | bytes 4194304 | tf_op jit(solution)/shard_map/all_to_all | solution.py:33
  470.8 49.4 %copy-start.7 = (bf16[1,1024,256]{2,1,0:T(8,128)(2,1)S(1)}, bf16[1,1024,256]{2,1,0:T(8,128)(2,1)}, u32[]{:S(2)}) copy-start(bf16[1,1024,256]{2,1,0:T(8,128)(2,1)} %param.10) | copy-start | bytes 1572868
  470.8 49.4 %copy-start.8 = (bf16[1,1024,256]{2,1,0:T(8,128)(2,1)S(1)}, bf16[1,1024,256]{2,1,0:T(8,128)(2,1)}, u32[]{:S(2)}) copy-start(bf16[1,1024,256]{2,1,0:T(8,128)(2,1)} %param.9) | copy-start | bytes 1572868
Sparse Core Ops, SparseCore 0:
  12.7 111.0 all-gather.4
  132.5 99.8 all-gather.6
  240.9 93.3 all-gather.8
  343.8 91.8 all-gather.10
where the time goes:
time: 530 us; the launch traced here: 528 us
  waiting for transfers between devices  341 us (64%)
  starting transfers between devices  66.8 us (13%)
  blocking collectives  52.6 us (10%)
  other arithmetic  35.3 us (7%)
  between operations  14.2 us (3%)
  matrix products  12.5 us (2%)
  local copies, waits for them, and re-layouts  6.03 us (1%)
    all_gather x4, waiting for transfers between devices, side_by_side(): out = lax.all_gather(both, axis, axis=dim, tiled=True)  270 us
    all_to_all x3, blocking collectives, from_everyone(): lax.all_to_all(jnp.broadcast_to(array[None], (length, *array.shape)), axi...  52.6 us
    all_to_all x5, waiting for transfers between devices, sent_and_summed(): lax.all_to_all(cut_along(array, dim, length), axis, 0, 0, tiled=True)  45 us
    all_to_all x5, starting transfers between devices, sent_and_summed(): lax.all_to_all(cut_along(array, dim, length), axis, 0, 0, tiled=True)  42.6 us
    ppermute x6, starting transfers between devices, shifted(): return lax.ppermute(block, axis, route)  17.3 us
    ppermute x6, waiting for transfers between devices, shifted(): return lax.ppermute(block, axis, route)  15.3 us
  transfers between devices with their start and end apart: 16, of which 11 were waited for; matrix products, arithmetic and copies ran while one was open for 8% of the time, Pallas kernels for 0%

commit v1 on v0

v1 whole, which is shorter than its diff:
```python
import functools

import jax
import jax.numpy as jnp
from jax import lax
from jax.experimental import pallas as pl
from jax.experimental.pallas import tpu as pltpu
from jax.sharding import PartitionSpec as P

EPSILON = 1e-06
MOMENTUM_RATE = 0.9
LEARNING_RATE = 0.05
MESH = pl.DeviceIdType.MESH
F32 = jnp.float32
BF16 = jnp.bfloat16

SIDE = 4
NEAR_LAST = (2, 1, 3, 0)
NEAR_FIRST = (0, 1, 3, 2)


def local_wait(ref, sem):
    pltpu.make_async_copy(ref, ref, sem).wait()


def kernel(
    w_in, new_in, mom_in, x_in, inc_in, g_in, loss_in, kept_in,
    f_out, b_out, w_out, m_out,
    w, x, kept, part, part_in, half, half_in, grad, f_own, b_own, f_send, b_send,
    inc, loss, scaled, p1, p1_in, p2, p2_in, kw, keep0, dw, dw_in, new, mom, w_new, m_new,
    load, fz_r, fz_s, fx_r, fx_s, kz_r, kz_s, kx_r, kx_s, rx_r, rx_s, rz_r, rz_s,
    p1_r, p1_s, p2_r, p2_s, g_r, g_s, dp_r, dp_s, out_sem,
):
    blocks, depth, own_cols = w.shape
    ticks, rows = x.shape[0], x.shape[2]
    extent = blocks * depth
    inv_root = 1.0 / float(extent) ** 0.5
    s, r, j = lax.axis_index("section"), lax.axis_index("dp"), lax.axis_index("tensor")
    sections, replicas = lax.axis_size("section"), lax.axis_size("dp")
    col, rank = lax.div(j, SIDE), lax.rem(j, SIDE)
    up, down = lax.rem(s + 1, sections), lax.rem(s + sections - 1, sections)
    is_first, is_last = s == 0, s == sections - 1

    def xs(e):
        return lax.rem(col + e + SIDE, SIDE)

    def zs(d):
        return lax.rem(rank + d + SIDE, SIDE)

    def remote(src, dst, send, recv, device):
        pltpu.make_async_remote_copy(
            src_ref=src, dst_ref=dst, send_sem=send, recv_sem=recv,
            device_id=device, device_id_type=MESH,
        ).start()

    barrier = pltpu.get_barrier_semaphore()
    peers = [(s, r, xs(e) * SIDE + rank) for e in range(1, SIDE)]
    peers += [(s, r, col * SIDE + zs(d)) for d in range(1, SIDE)]
    peers += [(q, r, col * SIDE + zs(d)) for q in (up, down) for d in range(SIDE)]
    peers += [(s, lax.rem(r + f, replicas), j) for f in range(1, replicas)]
    for peer in peers:
        pl.semaphore_signal(barrier, inc=1, device_id=peer, device_id_type=MESH)

    loads = [
        pltpu.make_async_copy(src, dst, load.at[i])
        for i, (src, dst) in enumerate([
            (x_in, x.at[0, j]), (g_in, grad.at[0]), (kept_in, kept.at[j]), (w_in, w),
            (inc_in, inc), (loss_in, loss), (new_in, new), (mom_in, mom),
        ])
    ]
    for copy in loads:
        copy.start()
    for copy in loads[:3]:
        copy.wait()
    pl.semaphore_wait(barrier, len(peers))

    for d in NEAR_LAST[:3]:
        remote(x.at[0, j], x.at[0, j], fz_s.at[0], fz_r.at[0, d], (s, r, col * SIDE + zs(d)))

    def kept_to_z(t):
        mine = kept.at[j, pl.ds(pl.multiple_of(t * rows, rows), rows), :]
        for d in NEAR_LAST[:3]:
            remote(mine, mine, kz_s.at[t], kz_r.at[t], (s, r, col * SIDE + zs(d)))

    def kept_to_x(t):
        span = pl.ds(pl.multiple_of(t * rows, rows), rows)
        local_wait(kept.at[pl.ds(0, SIDE - 1), span, :], kz_r.at[t])
        group = kept.at[pl.ds(col * SIDE, SIDE), span, :]
        for e in NEAR_LAST[:3]:
            remote(group, group, kx_s.at[t], kx_r.at[t], (s, r, xs(e) * SIDE + rank))

    loads[3].wait()
    loads[4].wait()
    loads[5].wait()

    row_id = lax.broadcasted_iota(jnp.int32, (rows, 128), 0)
    lane_id = lax.broadcasted_iota(jnp.int32, (rows, 128), 1)
    diagonal = row_id == lane_id

    def tick(t, carry):
        @pl.when(t > 0)
        def _():
            local_wait(grad.at[0], g_r.at[t])

        g = grad[t]
        for e in NEAR_LAST:
            for d in NEAR_LAST:
                k = xs(e) * SIDE + zs(d)
                term = lax.dot_general(
                    g, w[k], (((1,), (1,)), ((), ())), preferred_element_type=F32
                )
                part[t, k] = (term * inv_root).astype(BF16)
                if e:
                    remote(
                        part.at[t, k], part_in.at[t, d, e - 1], rx_s.at[t], rx_r.at[t, d],
                        (s, r, xs(e) * SIDE + rank),
                    )

        def pass_on(d):
            k = col * SIDE + zs(-d)
            for e in NEAR_LAST[:3]:
                remote(
                    x.at[t, k], x.at[t, k], fx_s.at[t], fx_r.at[t, d],
                    (s, r, xs(e) * SIDE + rank),
                )

        @pl.when(t > 0)
        def _():
            local_wait(x.at[t, 0], fz_r.at[t, 0])

        pass_on(0)

        @pl.when(t == 0)
        def _():
            kept_to_z(t)

        for d in (1, 3):
            local_wait(x.at[t, 0], fz_r.at[t, d])
            pass_on(d)

        def over_x(d):
            local_wait(part_in.at[t, d], rx_r.at[t, d])
            total = part[t, col * SIDE + zs(d)].astype(F32)
            for e in range(SIDE - 1):
                total += part_in[t, d, e].astype(F32)
            return total

        for d in (2, 1, 3):
            half[t, d - 1] = over_x(d).astype(BF16)
            remote(
                half.at[t, d - 1], half_in.at[t, d - 1], rz_s.at[t], rz_r.at[t],
                (s, r, col * SIDE + zs(d)),
            )
        keep0[...] = over_x(0)

        local_wait(x.at[t, 0], fz_r.at[t, 2])
        pass_on(2)

        @pl.when(t == 0)
        def _():
            kept_to_x(t)

        @pl.when(t < ticks - 1)
        def _():
            kept_to_z(t + 1)

        span = pl.ds(pl.multiple_of(t * rows, rows), rows)
        local_wait(kept.at[pl.ds(0, SIDE * (SIDE - 1)), span, :], kx_r.at[t])
        kept_product = jnp.zeros((rows, own_cols), F32)
        squares = jnp.zeros((rows, own_cols), F32)
        for k in range(blocks):
            block = kept[k, span, :]
            kept_product += jnp.dot(block, w[k], preferred_element_type=F32)
            wide = block.astype(F32)
            squares += wide * wide
        kept_scale = lax.rsqrt(jnp.sum(squares, axis=-1, keepdims=True) / extent + EPSILON)
        g_wide = grad[t].astype(F32)
        scaled[span, :] = (g_wide * kept_scale).astype(BF16)
        dots = jnp.sum(g_wide * kept_product, axis=-1, keepdims=True) * kept_scale * inv_root
        p1[t] = jnp.sum(jnp.where(diagonal, dots, 0.0), axis=0, keepdims=True)
        for e in NEAR_LAST[:3]:
            remote(
                p1.at[t], p1_in.at[t, e - 1], p1_s.at[t], p1_r.at[t],
                (s, r, xs(e) * SIDE + rank),
            )

        @pl.when(t == ticks - 1)
        def _():
            right = scaled[...]
            for f in (3, 2, 1, 0):
                owner = lax.rem(r + f, replicas)
                for c in range(SIDE):
                    k = owner * SIDE + c
                    term = lax.dot_general(
                        kept[k], right, (((0,), (0,)), ((), ())), preferred_element_type=F32
                    )
                    dw[k] = (term * inv_root).astype(BF16)
                if f:
                    remote(
                        dw.at[pl.ds(owner * SIDE, SIDE)], dw_in.at[f - 1], dp_s, dp_r.at[f - 1],
                        (s, owner, j),
                    )

        total = jnp.zeros((rows, own_cols), F32)
        squares = jnp.zeros((rows, own_cols), F32)
        for d in NEAR_FIRST:
            local_wait(x.at[t, pl.ds(0, SIDE - 1)], fx_r.at[t, d])
            for e in range(SIDE):
                k = xs(-e) * SIDE + zs(-d)
                block = x[t, k]
                total += jnp.dot(block, w[k], preferred_element_type=F32)
                wide = block.astype(F32)
                squares += wide * wide
        scale = lax.rsqrt(jnp.sum(squares, axis=-1, keepdims=True) / extent + EPSILON)
        result = (x[t, j].astype(F32) + total * scale * inv_root).astype(BF16)
        f_own[t] = result

        @pl.when(t < ticks - 1)
        def _():
            f_send[t] = jnp.where(is_last, inc[jnp.minimum(t, ticks - 2)], result)
            for d in NEAR_LAST:
                remote(
                    f_send.at[t], x.at[t + 1, j], fz_s.at[t + 1], fz_r.at[t + 1, d],
                    (up, r, col * SIDE + zs(d)),
                )

        local_wait(p1_in.at[t], p1_r.at[t])
        p2[t] = p1[t] + p1_in[t, 0] + p1_in[t, 1] + p1_in[t, 2]
        for d in NEAR_LAST[:3]:
            remote(
                p2.at[t], p2_in.at[t, d - 1], p2_s.at[t], p2_r.at[t],
                (s, r, col * SIDE + zs(d)),
            )

        @pl.when(t < ticks - 1)
        def _():
            kept_to_x(t + 1)

        local_wait(half_in.at[t], rz_r.at[t])
        branch = keep0[...]
        for d in range(SIDE - 1):
            branch += half_in[t, d].astype(F32)
        local_wait(p2_in.at[t], p2_r.at[t])
        line = p2[t] + p2_in[t, 0] + p2_in[t, 1] + p2_in[t, 2]
        inner = jnp.sum(jnp.where(diagonal, line, 0.0), axis=-1, keepdims=True) / extent
        hat = kept[j, span, :].astype(F32) * kept_scale
        back = (grad[t].astype(F32) + (branch - hat * inner) * kept_scale).astype(BF16)
        b_own[t] = back

        @pl.when(t < ticks - 1)
        def _():
            b_send[t] = jnp.where(is_first, loss[jnp.minimum(t, ticks - 2)], back)
            remote(b_send.at[t], grad.at[t + 1], g_s.at[t + 1], g_r.at[t + 1], (down, r, j))

        return carry

    lax.fori_loop(0, ticks, tick, 0)

    outs = [
        pltpu.make_async_copy(f_own, f_out, out_sem.at[0]),
        pltpu.make_async_copy(b_own, b_out, out_sem.at[1]),
    ]
    for copy in outs:
        copy.start()
    loads[6].wait()
    loads[7].wait()
    for f in range(replicas - 1):
        local_wait(dw_in.at[f], dp_r.at[f])
    for c in range(SIDE):
        summed = dw[r * SIDE + c].astype(F32)
        for f in range(replicas - 1):
            summed += dw_in[f, c].astype(F32)
        velocity = MOMENTUM_RATE * mom[c].astype(F32) + summed
        w_new[c] = (new[c].astype(F32) - LEARNING_RATE * velocity).astype(BF16)
        m_new[c] = velocity.astype(BF16)
    more = [
        pltpu.make_async_copy(w_new, w_out, out_sem.at[2]),
        pltpu.make_async_copy(m_new, m_out, out_sem.at[3]),
    ]
    for copy in more:
        copy.start()

    for t in range(ticks):
        local_wait(x.at[0, pl.ds(0, SIDE if t else SIDE - 1)], fz_s.at[t])
        local_wait(x.at[0, pl.ds(0, SIDE * (SIDE - 1))], fx_s.at[t])
        local_wait(x.at[0, pl.ds(0, SIDE - 1)], kz_s.at[t])
        local_wait(x.at[0, pl.ds(0, SIDE * (SIDE - 1))], kx_s.at[t])
        local_wait(x.at[0, pl.ds(0, SIDE * (SIDE - 1))], rx_s.at[t])
        local_wait(x.at[0, pl.ds(0, SIDE - 1)], rz_s.at[t])
        local_wait(p1_in.at[0], p1_s.at[t])
        local_wait(p2_in.at[0], p2_s.at[t])
        if t:
            local_wait(grad.at[0], g_s.at[t])
    local_wait(dw_in, dp_s)
    for copy in outs + more:
        copy.wait()


def body(
    shadow_weight_copy, newest_weight_version, momentum, pending_section_input,
    incoming_micro_input, pending_output_gradient, loss_gradient_rows, stashed,
):
    extent, cols = shadow_weight_copy.shape[1:]
    ticks, rows = stashed.shape[2:4]
    part_rows = newest_weight_version.shape[1]
    replicas = extent // part_rows
    blocks = extent // cols
    chunk = part_rows // SIDE

    vmem, dma = pltpu.VMEM, pltpu.SemaphoreType.DMA
    block = (rows, cols)
    scratch = [
        vmem((blocks, cols, cols), BF16),
        vmem((ticks, blocks, *block), BF16),
        vmem((blocks, ticks * rows, cols), BF16),
        vmem((ticks, blocks, *block), BF16),
        vmem((ticks, SIDE, SIDE - 1, *block), BF16),
        vmem((ticks, SIDE - 1, *block), BF16),
        vmem((ticks, SIDE - 1, *block), BF16),
        vmem((ticks, *block), BF16),
        vmem((ticks, *block), BF16),
        vmem((ticks, *block), BF16),
        vmem((ticks - 1, *block), BF16),
        vmem((ticks - 1, *block), BF16),
        vmem((ticks - 1, *block), BF16),
        vmem((ticks - 1, *block), BF16),
        vmem((ticks * rows, cols), BF16),
        vmem((ticks, 1, 128), F32),
        vmem((ticks, SIDE - 1, 1, 128), F32),
        vmem((ticks, 1, 128), F32),
        vmem((ticks, SIDE - 1, 1, 128), F32),
        vmem(block, F32),
        vmem(block, F32),
        vmem((blocks, cols, cols), BF16),
        vmem((replicas - 1, SIDE, chunk, cols), BF16),
        vmem((SIDE, chunk, cols), BF16),
        vmem((SIDE, chunk, cols), BF16),
        vmem((SIDE, chunk, cols), BF16),
        vmem((SIDE, chunk, cols), BF16),
        dma((8,)),
        dma((ticks, SIDE)), dma((ticks,)),
        dma((ticks, SIDE)), dma((ticks,)),
        dma((ticks,)), dma((ticks,)),
        dma((ticks,)), dma((ticks,)),
        dma((ticks, SIDE)), dma((ticks,)),
        dma((ticks,)), dma((ticks,)),
        dma((ticks,)), dma((ticks,)),
        dma((ticks,)), dma((ticks,)),
        dma((ticks,)), dma((ticks,)),
        dma((replicas - 1,)), dma,
        dma((4,)),
    ]
    any_space = pl.BlockSpec(memory_space=pl.ANY)
    shape = jax.ShapeDtypeStruct
    f_out, b_out, w_out, m_out = pl.pallas_call(
        kernel,
        name="window",
        out_shape=(
            shape((ticks, *block), BF16),
            shape((ticks, *block), BF16),
            shape((SIDE, chunk, cols), BF16),
            shape((SIDE, chunk, cols), BF16),
        ),
        in_specs=[any_space] * 8,
        out_specs=(any_space,) * 4,
        scratch_shapes=scratch,
        compiler_params=pltpu.CompilerParams(
            collective_id=0, has_side_effects=True, vmem_limit_bytes=60 * 1024 * 1024
        ),
    )(
        shadow_weight_copy.reshape(blocks, cols, cols),
        newest_weight_version.reshape(SIDE, chunk, cols),
        momentum.reshape(SIDE, chunk, cols),
        pending_section_input.reshape(block),
        incoming_micro_input.reshape(ticks - 1, *block),
        pending_output_gradient.reshape(block),
        loss_gradient_rows.reshape(ticks - 1, *block),
        stashed.reshape(ticks * rows, cols),
    )
    return (
        f_out[None, None],
        b_out[None, None],
        w_out.reshape(1, part_rows, cols),
        m_out.reshape(1, part_rows, cols),
    )


def solution(mesh):
    return jax.shard_map(
        body,
        mesh=mesh,
        in_specs=(
            P("section", None, "tensor"),
            P("section", "dp", "tensor"),
            P("section", "dp", "tensor"),
            P("dp", "section", None, "tensor"),
            P("dp", None, None, "tensor"),
            P("dp", "section", None, "tensor"),
            P("dp", None, None, "tensor"),
            P("dp", "section", None, None, "tensor"),
        ),
        out_specs=(
            P("dp", "section", None, None, "tensor"),
            P("dp", "section", None, None, "tensor"),
            P("section", "dp", "tensor"),
            P("section", "dp", "tensor"),
        ),
        check_vma=False,
    )
```

time: 530 us -> 183 us (0.35)
  waiting for transfers between devices: 341 us -> 0 us
  Pallas kernels: 0 us -> 175 us
  starting transfers between devices: 66.8 us -> 0 us
  blocking collectives: 52.6 us -> 0 us
  other arithmetic: 35.3 us -> 0 us
  between operations: 14.2 us -> 0.64 us
  matrix products: 12.5 us -> 0 us
    all_gather x4 -> x0, waiting for transfers between devices: 270 us -> none  [side_by_side(): out = lax.all_gather(both, axis, axis=dim, tiled=True)]
    pallas_call x0 -> x1, Pallas kernels: none -> 175 us  [body(): pl.pallas_call(kernel, name='window', out_shape=(shape((ticks, *block), B...]
    all_to_all x6 -> x0, waiting for transfers between devices: 55.1 us -> none  [the longest x5 45 us: sent_and_summed(): lax.all_to_all(cut_along(array, dim, length), axis, 0, 0, tiled=True)]
    all_to_all x3 -> x0, blocking collectives: 52.6 us -> none  [from_everyone(): lax.all_to_all(jnp.broadcast_to(array[None], (length, *array.shape)), axi...]
    all_to_all x6 -> x0, starting transfers between devices: 49.3 us -> none  [the longest x5 42.6 us: sent_and_summed(): lax.all_to_all(cut_along(array, dim, length), axis, 0, 0, tiled=True)]
    ppermute x6 -> x0, starting transfers between devices: 17.3 us -> none  [shifted(): return lax.ppermute(block, axis, route)]
    ppermute x6 -> x0, waiting for transfers between devices: 15.3 us -> none  [shifted(): return lax.ppermute(block, axis, route)]
    reduce_sum x17 -> x0, other arithmetic: 14.9 us -> none  [the longest x4 6.27 us: normalized(): jnp.mean(values * values, axis=-1, keepdims=True) + EPSILON]
  transfers between devices with their start and end apart: 16 -> 0, of which waited for: 11 -> 0; matrix products, arithmetic and copies ran while one was open for 8% -> 0% of each run, Pallas kernels for 0% -> 0%
where the time goes in v1:
time: 183 us; the launch traced here: 182 us
  Pallas kernels  175 us (96%)
  local copies, waits for them, and re-layouts  6.87 us (4%)
    pallas_call x1, Pallas kernels, body(): pl.pallas_call(kernel, name='window', out_shape=(shape((ticks, *block), B...  175 us
    unnamed x4, local copies, waits for them, and re-layouts  6.87 us

profile of v1, /device:TPU:1, one launch (start us, length us, event | category | flops | bytes accessed | tf_op | source)
XLA Modules:
  0.0 182.3 jit_solution(17370930662889630900)
XLA Ops:
  0.6 174.8 %window.1 = (bf16[4,64,256]{2,1,0:T(8,128)(2,1)}, bf16[4,64,256]{2,1,0:T(8,128)(2,1)}, bf16[4,256,256]{2,1,0:T(8,128)(2,1)}, bf16[4,256,256]{2,1,0:T(8,128)(2,1)}) custom-call(bf16[16,256,256]{2,1,0:T(8,128)(2,1)} %bitcast.12, bf16[4,256,256]{2,1,0:T(8,128)(2,1)} %bitcast.13, bf16[4,256,256]{2,1,0:T(8,128)(2,1)} %bitcast.14, bf16[64,256]{1,0:T(8,128)(2,1)} %bitcast.22, ...), custom_call_target="tpu_custom_call" | custom-call | tf_op jit(solution)/shard_map/window/pallas_call | solution.py:355
  175.4 1.6 copy.16
  177.0 1.6 copy.17
  178.6 1.9 %copy.18 = bf16[1,1024,256]{2,1,0:T(8,128)(2,1)} copy(bf16[1,1024,256]{2,1,0:T(8,128)(2,1)} %bitcast.16) | data formatting | bytes 1048576
  180.4 1.9 %copy.19 = bf16[1,1024,256]{2,1,0:T(8,128)(2,1)} copy(bf16[1,1024,256]{2,1,0:T(8,128)(2,1)} %bitcast.15) | data formatting | bytes 1048576

commit v2 on v1

--- a/solution.py
+++ b/solution.py
@@ -27,7 +27,7 @@
     w_in, new_in, mom_in, x_in, inc_in, g_in, loss_in, kept_in,
     f_out, b_out, w_out, m_out,
     w, x, kept, part, part_in, half, half_in, grad, f_own, b_own, f_send, b_send,
-    inc, loss, scaled, p1, p1_in, p2, p2_in, kw, keep0, dw, dw_in, new, mom, w_new, m_new,
+    inc, loss, scaled, p1, p1_in, p2, p2_in, kw, ks, keep0, dw, dw_in, new, mom, w_new, m_new,
     load, fz_r, fz_s, fx_r, fx_s, kz_r, kz_s, kx_r, kx_s, rx_r, rx_s, rz_r, rz_s,
     p1_r, p1_s, p2_r, p2_s, g_r, g_s, dp_r, dp_s, out_sem,
 ):
@@ -97,86 +97,25 @@
     lane_id = lax.broadcasted_iota(jnp.int32, (rows, 128), 1)
     diagonal = row_id == lane_id
 
-    def tick(t, carry):
-        @pl.when(t > 0)
-        def _():
-            local_wait(grad.at[0], g_r.at[t])
-
-        g = grad[t]
-        for e in NEAR_LAST:
-            for d in NEAR_LAST:
-                k = xs(e) * SIDE + zs(d)
-                term = lax.dot_general(
-                    g, w[k], (((1,), (1,)), ((), ())), preferred_element_type=F32
-                )
-                part[t, k] = (term * inv_root).astype(BF16)
-                if e:
-                    remote(
-                        part.at[t, k], part_in.at[t, d, e - 1], rx_s.at[t], rx_r.at[t, d],
-                        (s, r, xs(e) * SIDE + rank),
-                    )
-
-        def pass_on(d):
-            k = col * SIDE + zs(-d)
-            for e in NEAR_LAST[:3]:
-                remote(
-                    x.at[t, k], x.at[t, k], fx_s.at[t], fx_r.at[t, d],
-                    (s, r, xs(e) * SIDE + rank),
-                )
-
-        @pl.when(t > 0)
-        def _():
-            local_wait(x.at[t, 0], fz_r.at[t, 0])
-
-        pass_on(0)
-
-        @pl.when(t == 0)
-        def _():
-            kept_to_z(t)
-
-        for d in (1, 3):
-            local_wait(x.at[t, 0], fz_r.at[t, d])
-            pass_on(d)
-
-        def over_x(d):
-            local_wait(part_in.at[t, d], rx_r.at[t, d])
-            total = part[t, col * SIDE + zs(d)].astype(F32)
-            for e in range(SIDE - 1):
-                total += part_in[t, d, e].astype(F32)
-            return total
-
-        for d in (2, 1, 3):
-            half[t, d - 1] = over_x(d).astype(BF16)
-            remote(
-                half.at[t, d - 1], half_in.at[t, d - 1], rz_s.at[t], rz_r.at[t],
-                (s, r, col * SIDE + zs(d)),
-            )
-        keep0[...] = over_x(0)
-
-        local_wait(x.at[t, 0], fz_r.at[t, 2])
-        pass_on(2)
-
-        @pl.when(t == 0)
-        def _():
-            kept_to_x(t)
-
-        @pl.when(t < ticks - 1)
-        def _():
-            kept_to_z(t + 1)
-
+    def kept_products(t):
         span = pl.ds(pl.multiple_of(t * rows, rows), rows)
         local_wait(kept.at[pl.ds(0, SIDE * (SIDE - 1)), span, :], kx_r.at[t])
-        kept_product = jnp.zeros((rows, own_cols), F32)
+        product = jnp.zeros((rows, own_cols), F32)
         squares = jnp.zeros((rows, own_cols), F32)
         for k in range(blocks):
             block = kept[k, span, :]
-            kept_product += jnp.dot(block, w[k], preferred_element_type=F32)
+            product += jnp.dot(block, w[k], preferred_element_type=F32)
             wide = block.astype(F32)
             squares += wide * wide
-        kept_scale = lax.rsqrt(jnp.sum(squares, axis=-1, keepdims=True) / extent + EPSILON)
+        found = lax.rsqrt(jnp.sum(squares, axis=-1, keepdims=True) / extent + EPSILON)
+        kw[...] = product * (found * inv_root)
+        ks[...] = jnp.broadcast_to(found, (rows, 128))
+
+    def row_products(t):
+        span = pl.ds(pl.multiple_of(t * rows, rows), rows)
         g_wide = grad[t].astype(F32)
-        scaled[span, :] = (g_wide * kept_scale).astype(BF16)
-        dots = jnp.sum(g_wide * kept_product, axis=-1, keepdims=True) * kept_scale * inv_root
+        scaled[span, :] = (g_wide * ks[:, :1]).astype(BF16)
+        dots = jnp.sum(g_wide * kw[...], axis=-1, keepdims=True)
         p1[t] = jnp.sum(jnp.where(diagonal, dots, 0.0), axis=0, keepdims=True)
         for e in NEAR_LAST[:3]:
             remote(
@@ -184,10 +123,19 @@
                 (s, r, xs(e) * SIDE + rank),
             )
 
+    def tick(t, carry):
+        span = pl.ds(pl.multiple_of(t * rows, rows), rows)
+
+        @pl.when(t > 0)
+        def _():
+            kept_products(t)
+            local_wait(grad.at[0], g_r.at[t])
+            row_products(t)
+
         @pl.when(t == ticks - 1)
         def _():
             right = scaled[...]
-            for f in (3, 2, 1, 0):
+            for f in (2, 3, 1, 0):
                 owner = lax.rem(r + f, replicas)
                 for c in range(SIDE):
                     k = owner * SIDE + c
@@ -200,6 +148,65 @@
                         dw.at[pl.ds(owner * SIDE, SIDE)], dw_in.at[f - 1], dp_s, dp_r.at[f - 1],
                         (s, owner, j),
                     )
+
+        g = grad[t]
+        for d in NEAR_LAST:
+            for e in NEAR_LAST:
+                k = xs(e) * SIDE + zs(d)
+                term = lax.dot_general(
+                    g, w[k], (((1,), (1,)), ((), ())), preferred_element_type=F32
+                )
+                part[t, k] = (term * inv_root).astype(BF16)
+                if e:
+                    remote(
+                        part.at[t, k], part_in.at[t, d, e - 1], rx_s.at[t], rx_r.at[t, d],
+                        (s, r, xs(e) * SIDE + rank),
+                    )
+
+        def pass_on(d):
+            k = col * SIDE + zs(-d)
+            for e in NEAR_LAST[:3]:
+                remote(
+                    x.at[t, k], x.at[t, k], fx_s.at[t], fx_r.at[t, d],
+                    (s, r, xs(e) * SIDE + rank),
+                )
+
+        @pl.when(t > 0)
+        def _():
+            local_wait(x.at[t, 0], fz_r.at[t, 0])
+
+        pass_on(0)
+
+        @pl.when(t == 0)
+        def _():
+            kept_to_z(t)
+
+        def over_x(d):
+            local_wait(part_in.at[t, d], rx_r.at[t, d])
+            total = part[t, col * SIDE + zs(d)].astype(F32)
+            for e in range(SIDE - 1):
+                total += part_in[t, d, e].astype(F32)
+            return total
+
+        for d in (2, 1, 3):
+            half[t, d - 1] = over_x(d).astype(BF16)
+            remote(
+                half.at[t, d - 1], half_in.at[t, d - 1], rz_s.at[t], rz_r.at[t],
+                (s, r, col * SIDE + zs(d)),
+            )
+            if d != 2:
+                local_wait(x.at[t, 0], fz_r.at[t, d])
+                pass_on(d)
+        keep0[...] = over_x(0)
+
+        local_wait(x.at[t, 0], fz_r.at[t, 2])
+        pass_on(2)
+
+        @pl.when(t == 0)
+        def _():
+            kept_to_x(t)
+            kept_products(t)
+            row_products(t)
 
         total = jnp.zeros((rows, own_cols), F32)
         squares = jnp.zeros((rows, own_cols), F32)
@@ -223,6 +230,7 @@
                     f_send.at[t], x.at[t + 1, j], fz_s.at[t + 1], fz_r.at[t + 1, d],
                     (up, r, col * SIDE + zs(d)),
                 )
+            kept_to_z(t + 1)
 
         local_wait(p1_in.at[t], p1_r.at[t])
         p2[t] = p1[t] + p1_in[t, 0] + p1_in[t, 1] + p1_in[t, 2]
@@ -232,10 +240,6 @@
                 (s, r, col * SIDE + zs(d)),
             )
 
-        @pl.when(t < ticks - 1)
-        def _():
-            kept_to_x(t + 1)
-
         local_wait(half_in.at[t], rz_r.at[t])
         branch = keep0[...]
         for d in range(SIDE - 1):
@@ -243,6 +247,7 @@
         local_wait(p2_in.at[t], p2_r.at[t])
         line = p2[t] + p2_in[t, 0] + p2_in[t, 1] + p2_in[t, 2]
         inner = jnp.sum(jnp.where(diagonal, line, 0.0), axis=-1, keepdims=True) / extent
+        kept_scale = ks[:, :1]
         hat = kept[j, span, :].astype(F32) * kept_scale
         back = (grad[t].astype(F32) + (branch - hat * inner) * kept_scale).astype(BF16)
         b_own[t] = back
@@ -251,6 +256,7 @@
         def _():
             b_send[t] = jnp.where(is_first, loss[jnp.minimum(t, ticks - 2)], back)
             remote(b_send.at[t], grad.at[t + 1], g_s.at[t + 1], g_r.at[t + 1], (down, r, j))
+            kept_to_x(t + 1)
 
         return carry
 
@@ -296,6 +302,19 @@
         copy.wait()
 
 
+def hand_over(f_in, b_in, w_in, m_in, f_out, b_out, w_out, m_out, f, b, w, m, sem):
+    pairs = [(f_in, f, f_out), (b_in, b, b_out), (w_in, w, w_out), (m_in, m, m_out)]
+    reads = [pltpu.make_async_copy(a, v, sem.at[0, i]) for i, (a, v, _) in enumerate(pairs)]
+    writes = [pltpu.make_async_copy(v, o, sem.at[1, i]) for i, (_, v, o) in enumerate(pairs)]
+    for copy in reads:
+        copy.start()
+    for read, write in zip(reads, writes):
+        read.wait()
+        write.start()
+    for copy in writes:
+        copy.wait()
+
+
 def body(
     shadow_weight_copy, newest_weight_version, momentum, pending_section_input,
     incoming_micro_input, pending_output_gradient, loss_gradient_rows, stashed,
@@ -330,6 +349,7 @@
         vmem((ticks, 1, 128), F32),
         vmem((ticks, SIDE - 1, 1, 128), F32),
         vmem(block, F32),
+        vmem((rows, 128), F32),
         vmem(block, F32),
         vmem((blocks, cols, cols), BF16),
         vmem((replicas - 1, SIDE, chunk, cols), BF16),
@@ -377,6 +397,25 @@
         loss_gradient_rows.reshape(ticks - 1, *block),
         stashed.reshape(ticks * rows, cols),
     )
+    f_out, b_out, w_out, m_out = pl.pallas_call(
+        hand_over,
+        name="hand_over",
+        out_shape=(
+            shape((ticks, *block), BF16),
+            shape((ticks, *block), BF16),
+            shape((SIDE, chunk, cols), BF16),
+            shape((SIDE, chunk, cols), BF16),
+        ),
+        in_specs=[any_space] * 4,
+        out_specs=(any_space,) * 4,
+        scratch_shapes=[
+            vmem((ticks, *block), BF16),
+            vmem((ticks, *block), BF16),
+            vmem((SIDE, chunk, cols), BF16),
+            vmem((SIDE, chunk, cols), BF16),
+            dma((2, 4)),
+        ],
+    )(f_out, b_out, w_out, m_out)
     return (
         f_out[None, None],
         b_out[None, None],

time: 183 us -> 192 us (1.049)
  the two profiles are of different devices: /device:TPU:1 before, /device:TPU:152 now
where the time goes in v2:
time: 192 us
  Pallas kernels  192 us (100%)
    pallas_call x1, Pallas kernels, body(): pl.pallas_call(kernel, name='window', out_shape=(shape((ticks, *block), B...  189 us

profile of v2, /device:TPU:152, one launch (start us, length us, event | category | flops | bytes accessed | tf_op | source)
XLA Modules:
  0.0 192.2 jit_solution(8878498513807089961)
XLA Ops:
  0.6 189.3 %window.1 = (bf16[4,64,256]{2,1,0:T(8,128)(2,1)}, bf16[4,64,256]{2,1,0:T(8,128)(2,1)}, bf16[4,256,256]{2,1,0:T(8,128)(2,1)}, bf16[4,256,256]{2,1,0:T(8,128)(2,1)}) custom-call(bf16[16,256,256]{2,1,0:T(8,128)(2,1)} %bitcast.12, bf16[4,256,256]{2,1,0:T(8,128)(2,1)} %bitcast.13, bf16[4,256,256]{2,1,0:T(8,128)(2,1)} %bitcast.14, bf16[64,256]{1,0:T(8,128)(2,1)} %bitcast.18, ...), custom_call_target="tpu_custom_call" | custom-call | tf_op jit(solution)/shard_map/window/pallas_call | solution.py:375
  190.0 2.2 %hand_over.1 = (bf16[4,64,256]{2,1,0:T(8,128)(2,1)}, bf16[4,64,256]{2,1,0:T(8,128)(2,1)}, bf16[4,256,256]{2,1,0:T(8,128)(2,1)}, bf16[4,256,256]{2,1,0:T(8,128)(2,1)}) custom-call(bf16[4,64,256]{2,1,0:T(8,128)(2,1)} %get-tuple-element.12.f_in, bf16[4,64,256]{2,1,0:T(8,128)(2,1)} %get-tuple-element.13.b_in, bf16[4,256,256]{2,1,0:T(8,128)(2,1)} %get-tuple-element.14.w_in, ...), custom_call_target="tpu_custom_call" | custom-call | tf_op jit(solution)/shard_map/hand_over/pallas_call | solution.py:400

commit v3 on v2

--- a/solution.py
+++ b/solution.py
@@ -74,9 +74,6 @@
         copy.wait()
     pl.semaphore_wait(barrier, len(peers))
 
-    for d in NEAR_LAST[:3]:
-        remote(x.at[0, j], x.at[0, j], fz_s.at[0], fz_r.at[0, d], (s, r, col * SIDE + zs(d)))
-
     def kept_to_z(t):
         mine = kept.at[j, pl.ds(pl.multiple_of(t * rows, rows), rows), :]
         for d in NEAR_LAST[:3]:
@@ -88,6 +85,10 @@
         group = kept.at[pl.ds(col * SIDE, SIDE), span, :]
         for e in NEAR_LAST[:3]:
             remote(group, group, kx_s.at[t], kx_r.at[t], (s, r, xs(e) * SIDE + rank))
+
+    kept_to_z(0)
+    for d in NEAR_LAST[:3]:
+        remote(x.at[0, j], x.at[0, j], fz_s.at[0], fz_r.at[0, d], (s, r, col * SIDE + zs(d)))
 
     loads[3].wait()
     loads[4].wait()
@@ -123,6 +124,15 @@
                 (s, r, xs(e) * SIDE + rank),
             )
 
+    def row_products_over_x(t):
+        local_wait(p1_in.at[t], p1_r.at[t])
+        p2[t] = p1[t] + p1_in[t, 0] + p1_in[t, 1] + p1_in[t, 2]
+        for d in NEAR_LAST[:3]:
+            remote(
+                p2.at[t], p2_in.at[t, d - 1], p2_s.at[t], p2_r.at[t],
+                (s, r, col * SIDE + zs(d)),
+            )
+
     def tick(t, carry):
         span = pl.ds(pl.multiple_of(t * rows, rows), rows)
 
@@ -143,11 +153,10 @@
                         kept[k], right, (((0,), (0,)), ((), ())), preferred_element_type=F32
                     )
                     dw[k] = (term * inv_root).astype(BF16)
-                if f:
-                    remote(
-                        dw.at[pl.ds(owner * SIDE, SIDE)], dw_in.at[f - 1], dp_s, dp_r.at[f - 1],
-                        (s, owner, j),
-                    )
+                    if f:
+                        remote(
+                            dw.at[k], dw_in.at[f - 1, c], dp_s, dp_r.at[f - 1], (s, owner, j)
+                        )
 
         g = grad[t]
         for d in NEAR_LAST:
@@ -177,10 +186,6 @@
 
         pass_on(0)
 
-        @pl.when(t == 0)
-        def _():
-            kept_to_z(t)
-
         def over_x(d):
             local_wait(part_in.at[t, d], rx_r.at[t, d])
             total = part[t, col * SIDE + zs(d)].astype(F32)
@@ -199,14 +204,30 @@
                 pass_on(d)
         keep0[...] = over_x(0)
 
+        @pl.when(t == 0)
+        def _():
+            kept_to_x(0)
+            kept_to_z(1)
+
         local_wait(x.at[t, 0], fz_r.at[t, 2])
         pass_on(2)
 
         @pl.when(t == 0)
         def _():
-            kept_to_x(t)
-            kept_products(t)
-            row_products(t)
+            kept_products(0)
+            row_products(0)
+
+        @pl.when(t > 0)
+        def _():
+            row_products_over_x(t)
+
+        @pl.when((t > 0) & (t < ticks - 1))
+        def _():
+            kept_to_x(t + 1)
+
+        @pl.when((t > 0) & (t < ticks - 2))
+        def _():
+            kept_to_z(t + 2)
 
         total = jnp.zeros((rows, own_cols), F32)
         squares = jnp.zeros((rows, own_cols), F32)
@@ -230,15 +251,12 @@
                     f_send.at[t], x.at[t + 1, j], fz_s.at[t + 1], fz_r.at[t + 1, d],
                     (up, r, col * SIDE + zs(d)),
                 )
-            kept_to_z(t + 1)
-
-        local_wait(p1_in.at[t], p1_r.at[t])
-        p2[t] = p1[t] + p1_in[t, 0] + p1_in[t, 1] + p1_in[t, 2]
-        for d in NEAR_LAST[:3]:
-            remote(
-                p2.at[t], p2_in.at[t, d - 1], p2_s.at[t], p2_r.at[t],
-                (s, r, col * SIDE + zs(d)),
-            )
+
+        @pl.when(t == 0)
+        def _():
+            row_products_over_x(t)
+            kept_to_x(1)
+            kept_to_z(2)
 
         local_wait(half_in.at[t], rz_r.at[t])
         branch = keep0[...]
@@ -256,7 +274,6 @@
         def _():
             b_send[t] = jnp.where(is_first, loss[jnp.minimum(t, ticks - 2)], back)
             remote(b_send.at[t], grad.at[t + 1], g_s.at[t + 1], g_r.at[t + 1], (down, r, j))
-            kept_to_x(t + 1)
 
         return carry
 

time: 192 us -> 164 us (0.85)
  the two profiles are of different devices: /device:TPU:152 before, /device:TPU:64 now
where the time goes in v3:
time: 164 us
  Pallas kernels  163 us (99%)
    pallas_call x1, Pallas kernels, body(): pl.pallas_call(kernel, name='window', out_shape=(shape((ticks, *block), B...  161 us

profile of v3, /device:TPU:64, one launch (start us, length us, event | category | flops | bytes accessed | tf_op | source)
XLA Modules:
  0.0 164.1 jit_solution(14506237109181167411)
XLA Ops:
  0.6 161.2 %window.1 = (bf16[4,64,256]{2,1,0:T(8,128)(2,1)}, bf16[4,64,256]{2,1,0:T(8,128)(2,1)}, bf16[4,256,256]{2,1,0:T(8,128)(2,1)}, bf16[4,256,256]{2,1,0:T(8,128)(2,1)}) custom-call(bf16[16,256,256]{2,1,0:T(8,128)(2,1)} %bitcast.12, bf16[4,256,256]{2,1,0:T(8,128)(2,1)} %bitcast.13, bf16[4,256,256]{2,1,0:T(8,128)(2,1)} %bitcast.14, bf16[64,256]{1,0:T(8,128)(2,1)} %bitcast.18, ...), custom_call_target="tpu_custom_call" | custom-call | tf_op jit(solution)/shard_map/window/pallas_call | solution.py:392
  161.9 2.2 %hand_over.1 = (bf16[4,64,256]{2,1,0:T(8,128)(2,1)}, bf16[4,64,256]{2,1,0:T(8,128)(2,1)}, bf16[4,256,256]{2,1,0:T(8,128)(2,1)}, bf16[4,256,256]{2,1,0:T(8,128)(2,1)}) custom-call(bf16[4,64,256]{2,1,0:T(8,128)(2,1)} %get-tuple-element.12.f_in, bf16[4,64,256]{2,1,0:T(8,128)(2,1)} %get-tuple-element.13.b_in, bf16[4,256,256]{2,1,0:T(8,128)(2,1)} %get-tuple-element.14.w_in, ...), custom_call_target="tpu_custom_call" | custom-call | tf_op jit(solution)/shard_map/hand_over/pallas_call | solution.py:417

commit v4 on v2

v4 whole, which is shorter than its diff:
```python
import functools

import jax
import jax.numpy as jnp
from jax import lax
from jax.experimental import pallas as pl
from jax.experimental.pallas import tpu as pltpu
from jax.sharding import PartitionSpec as P

EPSILON = 1e-06
MOMENTUM_RATE = 0.9
LEARNING_RATE = 0.05
MESH = pl.DeviceIdType.MESH
F32 = jnp.float32
BF16 = jnp.bfloat16

SIDE = 4
NEAR_LAST = (2, 1, 3, 0)
NEAR_FIRST = (0, 1, 3, 2)


def local_wait(ref, sem):
    pltpu.make_async_copy(ref, ref, sem).wait()


def kernel(
    w_in, new_in, mom_in, x_in, inc_in, g_in, loss_in, kept_in,
    f_out, b_out, w_out, m_out,
    w, x, kept, part, part_in, half, half_in, grad, f_own, b_own, f_send, b_send,
    inc, loss, scaled, sq, sq_in, dot, dot_in, ks, keep0, rows_all, new, mom, w_new, m_new,
    load, fz_r, fz_s, fx_r, fx_s, kz_r, kz_s, rx_r, rx_s, rz_r, rz_s,
    sq_r, sq_s, dot_r, dot_s, g_r, g_s, sc_r, sc_s, az_r, az_s, ar_r, ar_s, al_r, al_s, out_sem,
):
    blocks, depth, own_cols = w.shape
    ticks, rows = x.shape[0], x.shape[2]
    extent = blocks * depth
    inv_root = 1.0 / float(extent) ** 0.5
    s, r, j = lax.axis_index("section"), lax.axis_index("dp"), lax.axis_index("tensor")
    sections, replicas = lax.axis_size("section"), lax.axis_size("dp")
    col, rank = lax.div(j, SIDE), lax.rem(j, SIDE)
    up, down = lax.rem(s + 1, sections), lax.rem(s + sections - 1, sections)
    is_first, is_last = s == 0, s == sections - 1
    place = lax.rem(col - r + SIDE, SIDE)

    def xs(e):
        return lax.rem(col + e + SIDE, SIDE)

    def zs(d):
        return lax.rem(rank + d + SIDE, SIDE)

    def x_peer(e):
        return (s, r, xs(e) * SIDE + rank)

    def z_peer(d):
        return (s, r, col * SIDE + zs(d))

    def remote(src, dst, send, recv, device):
        pltpu.make_async_remote_copy(
            src_ref=src, dst_ref=dst, send_sem=send, recv_sem=recv,
            device_id=device, device_id_type=MESH,
        ).start()

    barrier = pltpu.get_barrier_semaphore()
    peers = [(s, r, lax.rem(j + i, blocks)) for i in range(1, blocks)]
    peers += [
        (s, lax.rem(r + f, replicas), col * SIDE + zs(d))
        for f in range(1, SIDE) for d in range(SIDE)
    ]
    peers += [(q, r, col * SIDE + zs(d)) for q in (up, down) for d in range(SIDE)]
    for peer in peers:
        pl.semaphore_signal(barrier, inc=1, device_id=peer, device_id_type=MESH)

    loads = [
        pltpu.make_async_copy(src, dst, load.at[i])
        for i, (src, dst) in enumerate([
            (x_in, x.at[0, j]), (kept_in, kept.at[rank]), (g_in, grad.at[0]), (w_in, w),
            (inc_in, inc), (loss_in, loss), (new_in, new), (mom_in, mom),
        ])
    ]
    for copy in loads:
        copy.start()

    row_id = lax.broadcasted_iota(jnp.int32, (rows, 128), 0)
    lane_id = lax.broadcasted_iota(jnp.int32, (rows, 128), 1)
    diagonal = row_id == lane_id

    def to_line(column):
        return jnp.sum(jnp.where(diagonal, column, 0.0), axis=0, keepdims=True)

    def to_column(line):
        return jnp.sum(jnp.where(diagonal, line, 0.0), axis=-1, keepdims=True)

    def share(src, dst_of, send, recv):
        for i in range(1, blocks):
            remote(src, dst_of(i - 1), send, recv, (s, r, lax.rem(j + i, blocks)))

    def span(t):
        return pl.ds(pl.multiple_of(t * rows, rows), rows)

    for copy in loads[:3]:
        copy.wait()
    for t in range(ticks):
        wide = kept[rank, t * rows:(t + 1) * rows, :].astype(F32)
        sq[t] = to_line(jnp.sum(wide * wide, axis=-1, keepdims=True))
    pl.semaphore_wait(barrier, len(peers))

    for d in NEAR_LAST[:3]:
        remote(x.at[0, j], x.at[0, j], fz_s.at[0], fz_r.at[0, d], z_peer(d))

    def kept_to_z(t):
        mine = kept.at[rank, span(t), :]
        for d in NEAR_LAST[:3]:
            remote(mine, mine, kz_s.at[t], kz_r.at[t], z_peer(d))

    kept_to_z(0)
    share(sq, lambda i: sq_in.at[i], sq_s, sq_r)
    for copy in loads[3:6]:
        copy.wait()

    length = kept.shape[1] // 2

    def all_span(h):
        return pl.ds(h * length, length)

    def gather_z(h):
        mine = kept.at[rank, all_span(h), :]
        there = rows_all.at[rank, r, all_span(h), :]
        for d in NEAR_LAST[:3]:
            remote(mine, there, az_s.at[h], az_r.at[h], (s, col, col * SIDE + zs(d)))

        @pl.when(place != 0)
        def _():
            remote(mine, there, az_s.at[h], az_r.at[h], (s, col, j))

        @pl.when(place == 0)
        def _():
            pltpu.make_async_copy(mine, there, az_r.at[h]).start()

    def turn_right(h):
        group = rows_all.at[pl.ds(0, 2), :, all_span(h), :]
        remote(group, group, ar_s.at[h], ar_r.at[h], x_peer(1))

    def turn_left(h):
        group = rows_all.at[pl.ds(2, 2), :, all_span(h), :]
        remote(group, group, al_s.at[h], al_r.at[h], x_peer(-1))

    def wait_right(h):
        local_wait(rows_all.at[pl.ds(0, 2), :, all_span(h), :], ar_r.at[h])

    def wait_left(h):
        local_wait(rows_all.at[pl.ds(2, 2), :, all_span(h), :], al_r.at[h])

    def gather_x1(h):
        @pl.when(place == 0)
        def _():
            local_wait(rows_all.at[:, :, all_span(h), :], az_r.at[h])
            turn_right(h)
            turn_left(h)

    def gather_x2(h):
        @pl.when(place == 1)
        def _():
            wait_right(h)
            turn_right(h)

        @pl.when(place == 3)
        def _():
            wait_left(h)
            turn_left(h)

    def gather_x3(h):
        @pl.when(place == 2)
        def _():
            wait_right(h)
            wait_left(h)
            turn_right(h)
            turn_left(h)

    def gather_end(h):
        @pl.when(place == 1)
        def _():
            wait_left(h)

        @pl.when(place == 3)
        def _():
            wait_right(h)

    def scaled_rows(t):
        scaled[r, span(t), :] = (grad[t].astype(F32) * ks[t, :, :1]).astype(BF16)
        mine = scaled.at[r, span(t), :]
        for f in (2, 1, 3):
            remote(mine, mine, sc_s.at[t], sc_r.at[t], (s, lax.rem(r + f, replicas), j))

    def tick(t, carry):
        @pl.when(t > 0)
        def _():
            local_wait(grad.at[0], g_r.at[t])

        g = grad[t]
        for d in NEAR_LAST:
            for e in NEAR_LAST:
                k = xs(e) * SIDE + zs(d)
                term = lax.dot_general(
                    g, w[k], (((1,), (1,)), ((), ())), preferred_element_type=F32
                )
                part[t, k] = (term * inv_root).astype(BF16)
                if e:
                    remote(
                        part.at[t, k], part_in.at[t, d, e - 1], rx_s.at[t], rx_r.at[t, d],
                        x_peer(e),
                    )

        def pass_on(d):
            k = col * SIDE + zs(-d)
            for e in NEAR_LAST[:3]:
                remote(x.at[t, k], x.at[t, k], fx_s.at[t], fx_r.at[t, d], x_peer(e))

        @pl.when(t > 0)
        def _():
            local_wait(x.at[t, 0], fz_r.at[t, 0])

        pass_on(0)

        local_wait(kept.at[pl.ds(0, SIDE - 1), span(t), :], kz_r.at[t])

        def over_x(d):
            local_wait(part_in.at[t, d], rx_r.at[t, d])
            total = part[t, col * SIDE + zs(d)].astype(F32)
            for e in range(SIDE - 1):
                total += part_in[t, d, e].astype(F32)
            return total

        products = jnp.zeros((rows, own_cols), F32)
        for d in (2, 1, 3):
            total = over_x(d)
            half[t, d - 1] = total.astype(BF16)
            remote(half.at[t, d - 1], half_in.at[t, d - 1], rz_s.at[t], rz_r.at[t], z_peer(d))
            products += total * kept[zs(d), span(t), :].astype(F32)
            if d != 2:
                local_wait(x.at[t, 0], fz_r.at[t, d])
                pass_on(d)
        total = over_x(0)
        keep0[...] = total
        products += total * kept[rank, span(t), :].astype(F32)
        dot[t] = to_line(jnp.sum(products, axis=-1, keepdims=True))
        share(dot.at[t], lambda i: dot_in.at[t, i], dot_s.at[t], dot_r.at[t])

        local_wait(x.at[t, 0], fz_r.at[t, 2])
        pass_on(2)

        @pl.when(t < ticks - 1)
        def _():
            kept_to_z(t + 1)

        @pl.when(t == 0)
        def _():
            gather_z(0)

        @pl.when(t == 1)
        def _():
            gather_x1(0)

        @pl.when(t == 2)
        def _():
            gather_x2(0)

        @pl.when(t == 3)
        def _():
            scaled_rows(t)
            gather_x3(0)
            gather_x3(1)

        total = jnp.zeros((rows, own_cols), F32)
        squares = jnp.zeros((rows, own_cols), F32)
        for d in NEAR_FIRST:
            local_wait(x.at[t, pl.ds(0, SIDE - 1)], fx_r.at[t, d])
            for e in range(SIDE):
                k = xs(-e) * SIDE + zs(-d)
                block = x[t, k]
                total += jnp.dot(block, w[k], preferred_element_type=F32)
                wide = block.astype(F32)
                squares += wide * wide
        scale = lax.rsqrt(jnp.sum(squares, axis=-1, keepdims=True) / extent + EPSILON)
        result = (x[t, j].astype(F32) + total * scale * inv_root).astype(BF16)
        f_own[t] = result

        @pl.when(t < ticks - 1)
        def _():
            f_send[t] = jnp.where(is_last, inc[jnp.minimum(t, ticks - 2)], result)
            for d in NEAR_LAST:
                remote(
                    f_send.at[t], x.at[t + 1, j], fz_s.at[t + 1], fz_r.at[t + 1, d],
                    (up, r, col * SIDE + zs(d)),
                )

        @pl.when(t == 0)
        def _():
            gather_z(1)
            local_wait(sq_in, sq_r)
            lines = sq[...] + jnp.sum(sq_in[...], axis=0)
            for u in range(ticks):
                found = lax.rsqrt(to_column(lines[u]) / extent + EPSILON)
                ks[u] = jnp.broadcast_to(found, (rows, 128))

        @pl.when(t < ticks - 1)
        def _():
            scaled_rows(t)

        @pl.when(t == 1)
        def _():
            gather_x1(1)

        @pl.when(t == 2)
        def _():
            gather_x2(1)

        local_wait(half_in.at[t], rz_r.at[t])
        branch = keep0[...]
        for d in range(SIDE - 1):
            branch += half_in[t, d].astype(F32)
        local_wait(dot_in.at[t], dot_r.at[t])
        kept_scale = ks[t, :, :1]
        inner = to_column(dot[t] + jnp.sum(dot_in[t], axis=0)) * kept_scale / extent
        hat = kept[rank, span(t), :].astype(F32) * kept_scale
        back = (grad[t].astype(F32) + (branch - hat * inner) * kept_scale).astype(BF16)
        b_own[t] = back

        @pl.when(t < ticks - 1)
        def _():
            b_send[t] = jnp.where(is_first, loss[jnp.minimum(t, ticks - 2)], back)
            remote(b_send.at[t], grad.at[t + 1], g_s.at[t + 1], g_r.at[t + 1], (down, r, j))

        return carry

    lax.fori_loop(0, ticks, tick, 0)

    outs = [
        pltpu.make_async_copy(f_own, f_out, out_sem.at[0]),
        pltpu.make_async_copy(b_own, b_out, out_sem.at[1]),
    ]
    for copy in outs:
        copy.start()
    loads[6].wait()
    loads[7].wait()
    for t in range(ticks):
        local_wait(scaled.at[pl.ds(0, SIDE - 1), span(t), :], sc_r.at[t])
    gather_end(0)
    gather_end(1)
    for c in range(SIDE):
        summed = jnp.zeros((depth, own_cols), F32)
        for q in range(SIDE):
            summed += lax.dot_general(
                rows_all[c, q], scaled[q], (((0,), (0,)), ((), ())), preferred_element_type=F32
            )
        velocity = MOMENTUM_RATE * mom[c].astype(F32) + summed * inv_root
        w_new[c] = (new[c].astype(F32) - LEARNING_RATE * velocity).astype(BF16)
        m_new[c] = velocity.astype(BF16)
    more = [
        pltpu.make_async_copy(w_new, w_out, out_sem.at[2]),
        pltpu.make_async_copy(m_new, m_out, out_sem.at[3]),
    ]
    for copy in more:
        copy.start()

    local_wait(sq_in, sq_s)
    for t in range(ticks):
        local_wait(x.at[0, pl.ds(0, SIDE if t else SIDE - 1)], fz_s.at[t])
        local_wait(x.at[0, pl.ds(0, SIDE * (SIDE - 1))], fx_s.at[t])
        local_wait(x.at[0, pl.ds(0, SIDE - 1)], kz_s.at[t])
        local_wait(x.at[0, pl.ds(0, SIDE * (SIDE - 1))], rx_s.at[t])
        local_wait(x.at[0, pl.ds(0, SIDE - 1)], rz_s.at[t])
        local_wait(x.at[0, pl.ds(0, SIDE - 1)], sc_s.at[t])
        local_wait(dot_in.at[0], dot_s.at[t])
        if t:
            local_wait(grad.at[0], g_s.at[t])
    for h in range(2):
        local_wait(rows_all.at[0, pl.ds(0, SIDE - 1), all_span(h), :], az_s.at[h])

        @pl.when(place != 0)
        def _():
            local_wait(rows_all.at[0, 0, all_span(h), :], az_s.at[h])

        @pl.when(place != 3)
        def _():
            local_wait(rows_all.at[pl.ds(0, 2), :, all_span(h), :], ar_s.at[h])

        @pl.when(place != 1)
        def _():
            local_wait(rows_all.at[pl.ds(2, 2), :, all_span(h), :], al_s.at[h])

    for copy in outs + more:
        copy.wait()


def hand_over(f_in, b_in, w_in, m_in, f_out, b_out, w_out, m_out, f, b, w, m, sem):
    pairs = [(f_in, f, f_out), (b_in, b, b_out), (w_in, w, w_out), (m_in, m, m_out)]
    reads = [pltpu.make_async_copy(a, v, sem.at[0, i]) for i, (a, v, _) in enumerate(pairs)]
    writes = [pltpu.make_async_copy(v, o, sem.at[1, i]) for i, (_, v, o) in enumerate(pairs)]
    for copy in reads:
        copy.start()
    for read, write in zip(reads, writes):
        read.wait()
        write.start()
    for copy in writes:
        copy.wait()


def body(
    shadow_weight_copy, newest_weight_version, momentum, pending_section_input,
    incoming_micro_input, pending_output_gradient, loss_gradient_rows, stashed,
):
    extent, cols = shadow_weight_copy.shape[1:]
    ticks, rows = stashed.shape[2:4]
    part_rows = newest_weight_version.shape[1]
    replicas = extent // part_rows
    blocks = extent // cols
    chunk = part_rows // SIDE

    vmem, dma = pltpu.VMEM, pltpu.SemaphoreType.DMA
    block = (rows, cols)
    scratch = [
        vmem((blocks, cols, cols), BF16),
        vmem((ticks, blocks, *block), BF16),
        vmem((SIDE, ticks * rows, cols), BF16),
        vmem((ticks, blocks, *block), BF16),
        vmem((ticks, SIDE, SIDE - 1, *block), BF16),
        vmem((ticks, SIDE - 1, *block), BF16),
        vmem((ticks, SIDE - 1, *block), BF16),
        vmem((ticks, *block), BF16),
        vmem((ticks, *block), BF16),
        vmem((ticks, *block), BF16),
        vmem((ticks - 1, *block), BF16),
        vmem((ticks - 1, *block), BF16),
        vmem((ticks - 1, *block), BF16),
        vmem((ticks - 1, *block), BF16),
        vmem((replicas, ticks * rows, cols), BF16),
        vmem((ticks, 1, 128), F32),
        vmem((blocks - 1, ticks, 1, 128), F32),
        vmem((ticks, 1, 128), F32),
        vmem((ticks, blocks - 1, 1, 128), F32),
        vmem((ticks, rows, 128), F32),
        vmem(block, F32),
        vmem((SIDE, replicas, ticks * rows, cols), BF16),
        vmem((SIDE, chunk, cols), BF16),
        vmem((SIDE, chunk, cols), BF16),
        vmem((SIDE, chunk, cols), BF16),
        vmem((SIDE, chunk, cols), BF16),
        dma((8,)),
        dma((ticks, SIDE)), dma((ticks,)),
        dma((ticks, SIDE)), dma((ticks,)),
        dma((ticks,)), dma((ticks,)),
        dma((ticks, SIDE)), dma((ticks,)),
        dma((ticks,)), dma((ticks,)),
        dma, dma,
        dma((ticks,)), dma((ticks,)),
        dma((ticks,)), dma((ticks,)),
        dma((ticks,)), dma((ticks,)),
        dma((2,)), dma((2,)),
        dma((2,)), dma((2,)),
        dma((2,)), dma((2,)),
        dma((4,)),
    ]
    any_space = pl.BlockSpec(memory_space=pl.ANY)
    shape = jax.ShapeDtypeStruct
    f_out, b_out, w_out, m_out = pl.pallas_call(
        kernel,
        name="window",
        out_shape=(
            shape((ticks, *block), BF16),
            shape((ticks, *block), BF16),
            shape((SIDE, chunk, cols), BF16),
            shape((SIDE, chunk, cols), BF16),
        ),
        in_specs=[any_space] * 8,
        out_specs=(any_space,) * 4,
        scratch_shapes=scratch,
        compiler_params=pltpu.CompilerParams(
            collective_id=0, has_side_effects=True, vmem_limit_bytes=60 * 1024 * 1024
        ),
    )(
        shadow_weight_copy.reshape(blocks, cols, cols),
        newest_weight_version.reshape(SIDE, chunk, cols),
        momentum.reshape(SIDE, chunk, cols),
        pending_section_input.reshape(block),
        incoming_micro_input.reshape(ticks - 1, *block),
        pending_output_gradient.reshape(block),
        loss_gradient_rows.reshape(ticks - 1, *block),
        stashed.reshape(ticks * rows, cols),
    )
    f_out, b_out, w_out, m_out = pl.pallas_call(
        hand_over,
        name="hand_over",
        out_shape=(
            shape((ticks, *block), BF16),
            shape((ticks, *block), BF16),
            shape((SIDE, chunk, cols), BF16),
            shape((SIDE, chunk, cols), BF16),
        ),
        in_specs=[any_space] * 4,
        out_specs=(any_space,) * 4,
        scratch_shapes=[
            vmem((ticks, *block), BF16),
            vmem((ticks, *block), BF16),
            vmem((SIDE, chunk, cols), BF16),
            vmem((SIDE, chunk, cols), BF16),
            dma((2, 4)),
        ],
    )(f_out, b_out, w_out, m_out)
    return (
        f_out[None, None],
        b_out[None, None],
        w_out.reshape(1, part_rows, cols),
        m_out.reshape(1, part_rows, cols),
    )


def solution(mesh):
    return jax.shard_map(
        body,
        mesh=mesh,
        in_specs=(
            P("section", None, "tensor"),
            P("section", "dp", "tensor"),
            P("section", "dp", "tensor"),
            P("dp", "section", None, "tensor"),
            P("dp", None, None, "tensor"),
            P("dp", "section", None, "tensor"),
            P("dp", None, None, "tensor"),
            P("dp", "section", None, None, "tensor"),
        ),
        out_specs=(
            P("dp", "section", None, None, "tensor"),
            P("dp", "section", None, None, "tensor"),
            P("section", "dp", "tensor"),
            P("section", "dp", "tensor"),
        ),
        check_vma=False,
    )
```

time: 192 us -> 198 us (1.031)
  the two profiles are of different devices: /device:TPU:152 before, /device:TPU:73 now
where the time goes in v4:
time: 198 us
  Pallas kernels  197 us (99%)
    pallas_call x1, Pallas kernels, body(): pl.pallas_call(kernel, name='window', out_shape=(shape((ticks, *block), B...  195 us

profile of v4, /device:TPU:73, one launch (start us, length us, event | category | flops | bytes accessed | tf_op | source)
XLA Modules:
  0.0 198.1 jit_solution(17035153369012308596)
XLA Ops:
  0.6 195.2 %window.1 = (bf16[4,64,256]{2,1,0:T(8,128)(2,1)}, bf16[4,64,256]{2,1,0:T(8,128)(2,1)}, bf16[4,256,256]{2,1,0:T(8,128)(2,1)}, bf16[4,256,256]{2,1,0:T(8,128)(2,1)}) custom-call(bf16[16,256,256]{2,1,0:T(8,128)(2,1)} %bitcast.12, bf16[4,256,256]{2,1,0:T(8,128)(2,1)} %bitcast.13, bf16[4,256,256]{2,1,0:T(8,128)(2,1)} %bitcast.14, bf16[64,256]{1,0:T(8,128)(2,1)} %bitcast.18, ...), custom_call_target="tpu_custom_call" | custom-call | tf_op jit(solution)/shard_map/window/pallas_call | solution.py:465
  195.8 2.2 %hand_over.1 = (bf16[4,64,256]{2,1,0:T(8,128)(2,1)}, bf16[4,64,256]{2,1,0:T(8,128)(2,1)}, bf16[4,256,256]{2,1,0:T(8,128)(2,1)}, bf16[4,256,256]{2,1,0:T(8,128)(2,1)}) custom-call(bf16[4,64,256]{2,1,0:T(8,128)(2,1)} %get-tuple-element.12.f_in, bf16[4,64,256]{2,1,0:T(8,128)(2,1)} %get-tuple-element.13.b_in, bf16[4,256,256]{2,1,0:T(8,128)(2,1)} %get-tuple-element.14.w_in, ...), custom_call_target="tpu_custom_call" | custom-call | tf_op jit(solution)/shard_map/hand_over/pallas_call | solution.py:490

commit v5 on v3

--- a/solution.py
+++ b/solution.py
@@ -27,9 +27,9 @@
     w_in, new_in, mom_in, x_in, inc_in, g_in, loss_in, kept_in,
     f_out, b_out, w_out, m_out,
     w, x, kept, part, part_in, half, half_in, grad, f_own, b_own, f_send, b_send,
-    inc, loss, scaled, p1, p1_in, p2, p2_in, kw, ks, keep0, dw, dw_in, new, mom, w_new, m_new,
+    inc, loss, scaled, p1, p1_in, p2, p2_in, kw, ks, keep0, dw, dw_in, own_sum, kept_pair, scaled_pair, new, mom, w_new, m_new,
     load, fz_r, fz_s, fx_r, fx_s, kz_r, kz_s, kx_r, kx_s, rx_r, rx_s, rz_r, rz_s,
-    p1_r, p1_s, p2_r, p2_s, g_r, g_s, dp_r, dp_s, out_sem,
+    p1_r, p1_s, p2_r, p2_s, g_r, g_s, pk_r, pk_s, ps_r, ps_s, dp_r, dp_s, out_sem,
 ):
     blocks, depth, own_cols = w.shape
     ticks, rows = x.shape[0], x.shape[2]
@@ -40,6 +40,9 @@
     col, rank = lax.div(j, SIDE), lax.rem(j, SIDE)
     up, down = lax.rem(s + 1, sections), lax.rem(s + sections - 1, sections)
     is_first, is_last = s == 0, s == sections - 1
+    pair = r + 1 - 2 * lax.rem(r, 2)
+    far = lax.rem(r + 2, replicas)
+    beyond = lax.rem(pair + 2, replicas)
 
     def xs(e):
         return lax.rem(col + e + SIDE, SIDE)
@@ -101,6 +104,11 @@
     def kept_products(t):
         span = pl.ds(pl.multiple_of(t * rows, rows), rows)
         local_wait(kept.at[pl.ds(0, SIDE * (SIDE - 1)), span, :], kx_r.at[t])
+        for i, owner in ((1, beyond), (0, pair)):
+            remote(
+                kept.at[pl.ds(owner * SIDE, SIDE), span, :], kept_pair.at[i, :, span, :],
+                pk_s.at[t], pk_r.at[t], (s, pair, j),
+            )
         product = jnp.zeros((rows, own_cols), F32)
         squares = jnp.zeros((rows, own_cols), F32)
         for k in range(blocks):
@@ -116,6 +124,9 @@
         span = pl.ds(pl.multiple_of(t * rows, rows), rows)
         g_wide = grad[t].astype(F32)
         scaled[span, :] = (g_wide * ks[:, :1]).astype(BF16)
+        remote(
+            scaled.at[span, :], scaled_pair.at[span, :], ps_s.at[t], ps_r.at[t], (s, pair, j)
+        )
         dots = jnp.sum(g_wide * kw[...], axis=-1, keepdims=True)
         p1[t] = jnp.sum(jnp.where(diagonal, dots, 0.0), axis=0, keepdims=True)
         for e in NEAR_LAST[:3]:
@@ -133,6 +144,16 @@
                 (s, r, col * SIDE + zs(d)),
             )
 
+    def pair_gradient(owner, i, c):
+        over_rows = (((0,), (0,)), ((), ()))
+        term = lax.dot_general(
+            kept[owner * SIDE + c], scaled[...], over_rows, preferred_element_type=F32
+        )
+        term += lax.dot_general(
+            kept_pair[i, c], scaled_pair[...], over_rows, preferred_element_type=F32
+        )
+        return term * inv_root
+
     def tick(t, carry):
         span = pl.ds(pl.multiple_of(t * rows, rows), rows)
 
@@ -141,22 +162,6 @@
             kept_products(t)
             local_wait(grad.at[0], g_r.at[t])
             row_products(t)
-
-        @pl.when(t == ticks - 1)
-        def _():
-            right = scaled[...]
-            for f in (2, 3, 1, 0):
-                owner = lax.rem(r + f, replicas)
-                for c in range(SIDE):
-                    k = owner * SIDE + c
-                    term = lax.dot_general(
-                        kept[k], right, (((0,), (0,)), ((), ())), preferred_element_type=F32
-                    )
-                    dw[k] = (term * inv_root).astype(BF16)
-                    if f:
-                        remote(
-                            dw.at[k], dw_in.at[f - 1, c], dp_s, dp_r.at[f - 1], (s, owner, j)
-                        )
 
         g = grad[t]
         for d in NEAR_LAST:
@@ -186,6 +191,16 @@
 
         pass_on(0)
 
+        @pl.when(t == ticks - 1)
+        def _():
+            for u in range(ticks):
+                rows_u = pl.ds(u * rows, rows)
+                local_wait(kept_pair.at[:, :, rows_u, :], pk_r.at[u])
+                local_wait(scaled_pair.at[rows_u, :], ps_r.at[u])
+            for c in range(SIDE):
+                dw[c] = pair_gradient(far, 1, c).astype(BF16)
+                remote(dw.at[c], dw_in.at[c], dp_s, dp_r, (s, far, j))
+
         def over_x(d):
             local_wait(part_in.at[t, d], rx_r.at[t, d])
             total = part[t, col * SIDE + zs(d)].astype(F32)
@@ -287,12 +302,11 @@
         copy.start()
     loads[6].wait()
     loads[7].wait()
-    for f in range(replicas - 1):
-        local_wait(dw_in.at[f], dp_r.at[f])
     for c in range(SIDE):
-        summed = dw[r * SIDE + c].astype(F32)
-        for f in range(replicas - 1):
-            summed += dw_in[f, c].astype(F32)
+        own_sum[c] = pair_gradient(r, 0, c)
+    local_wait(dw_in, dp_r)
+    for c in range(SIDE):
+        summed = own_sum[c] + dw_in[c].astype(F32)
         velocity = MOMENTUM_RATE * mom[c].astype(F32) + summed
         w_new[c] = (new[c].astype(F32) - LEARNING_RATE * velocity).astype(BF16)
         m_new[c] = velocity.astype(BF16)
@@ -312,9 +326,11 @@
         local_wait(x.at[0, pl.ds(0, SIDE - 1)], rz_s.at[t])
         local_wait(p1_in.at[0], p1_s.at[t])
         local_wait(p2_in.at[0], p2_s.at[t])
+        local_wait(x.at[0, pl.ds(0, 2 * SIDE)], pk_s.at[t])
+        local_wait(grad.at[0], ps_s.at[t])
         if t:
             local_wait(grad.at[0], g_s.at[t])
-    local_wait(dw_in, dp_s)
+    local_wait(dw, dp_s)
     for copy in outs + more:
         copy.wait()
 
@@ -368,8 +384,11 @@
         vmem(block, F32),
         vmem((rows, 128), F32),
         vmem(block, F32),
-        vmem((blocks, cols, cols), BF16),
-        vmem((replicas - 1, SIDE, chunk, cols), BF16),
+        vmem((SIDE, chunk, cols), BF16),
+        vmem((SIDE, chunk, cols), BF16),
+        vmem((SIDE, chunk, cols), F32),
+        vmem((2, SIDE, ticks * rows, cols), BF16),
+        vmem((ticks * rows, cols), BF16),
         vmem((SIDE, chunk, cols), BF16),
         vmem((SIDE, chunk, cols), BF16),
         vmem((SIDE, chunk, cols), BF16),
@@ -384,7 +403,9 @@
         dma((ticks,)), dma((ticks,)),
         dma((ticks,)), dma((ticks,)),
         dma((ticks,)), dma((ticks,)),
-        dma((replicas - 1,)), dma,
+        dma((ticks,)), dma((ticks,)),
+        dma((ticks,)), dma((ticks,)),
+        dma, dma,
         dma((4,)),
     ]
     any_space = pl.BlockSpec(memory_space=pl.ANY)

time: 164 us -> 163 us (level)
  the two profiles are of different devices: /device:TPU:64 before, /device:TPU:1 now
where the time goes in v5:
time: 163 us; the launch traced here: 160 us
  Pallas kernels  159 us (98%)
    pallas_call x1, Pallas kernels, body(): pl.pallas_call(kernel, name='window', out_shape=(shape((ticks, *block), B...  157 us

profile of v5, /device:TPU:1, one launch (start us, length us, event | category | flops | bytes accessed | tf_op | source)
XLA Modules:
  0.0 160.0 jit_solution(8474404756342189740)
XLA Ops:
  0.6 157.2 %window.1 = (bf16[4,64,256]{2,1,0:T(8,128)(2,1)}, bf16[4,64,256]{2,1,0:T(8,128)(2,1)}, bf16[4,256,256]{2,1,0:T(8,128)(2,1)}, bf16[4,256,256]{2,1,0:T(8,128)(2,1)}) custom-call(bf16[16,256,256]{2,1,0:T(8,128)(2,1)} %bitcast.12, bf16[4,256,256]{2,1,0:T(8,128)(2,1)} %bitcast.13, bf16[4,256,256]{2,1,0:T(8,128)(2,1)} %bitcast.14, bf16[64,256]{1,0:T(8,128)(2,1)} %bitcast.18, ...), custom_call_target="tpu_custom_call" | custom-call | tf_op jit(solution)/shard_map/window/pallas_call | solution.py:413
  157.8 2.2 %hand_over.1 = (bf16[4,64,256]{2,1,0:T(8,128)(2,1)}, bf16[4,64,256]{2,1,0:T(8,128)(2,1)}, bf16[4,256,256]{2,1,0:T(8,128)(2,1)}, bf16[4,256,256]{2,1,0:T(8,128)(2,1)}) custom-call(bf16[4,64,256]{2,1,0:T(8,128)(2,1)} %get-tuple-element.12.f_in, bf16[4,64,256]{2,1,0:T(8,128)(2,1)} %get-tuple-element.13.b_in, bf16[4,256,256]{2,1,0:T(8,128)(2,1)} %get-tuple-element.14.w_in, ...), custom_call_target="tpu_custom_call" | custom-call | tf_op jit(solution)/shard_map/hand_over/pallas_call | solution.py:438

commit v6 on v5

--- a/solution.py
+++ b/solution.py
@@ -101,14 +101,17 @@
     lane_id = lax.broadcasted_iota(jnp.int32, (rows, 128), 1)
     diagonal = row_id == lane_id
 
-    def kept_products(t):
+    def kept_to_pair(t):
         span = pl.ds(pl.multiple_of(t * rows, rows), rows)
-        local_wait(kept.at[pl.ds(0, SIDE * (SIDE - 1)), span, :], kx_r.at[t])
         for i, owner in ((1, beyond), (0, pair)):
             remote(
                 kept.at[pl.ds(owner * SIDE, SIDE), span, :], kept_pair.at[i, :, span, :],
                 pk_s.at[t], pk_r.at[t], (s, pair, j),
             )
+
+    def kept_products(t):
+        span = pl.ds(pl.multiple_of(t * rows, rows), rows)
+        local_wait(kept.at[pl.ds(0, SIDE * (SIDE - 1)), span, :], kx_r.at[t])
         product = jnp.zeros((rows, own_cols), F32)
         squares = jnp.zeros((rows, own_cols), F32)
         for k in range(blocks):
@@ -160,6 +163,11 @@
         @pl.when(t > 0)
         def _():
             kept_products(t)
+
+            @pl.when(t == ticks - 1)
+            def _():
+                kept_to_pair(t)
+
             local_wait(grad.at[0], g_r.at[t])
             row_products(t)
 
@@ -191,16 +199,6 @@
 
         pass_on(0)
 
-        @pl.when(t == ticks - 1)
-        def _():
-            for u in range(ticks):
-                rows_u = pl.ds(u * rows, rows)
-                local_wait(kept_pair.at[:, :, rows_u, :], pk_r.at[u])
-                local_wait(scaled_pair.at[rows_u, :], ps_r.at[u])
-            for c in range(SIDE):
-                dw[c] = pair_gradient(far, 1, c).astype(BF16)
-                remote(dw.at[c], dw_in.at[c], dp_s, dp_r, (s, far, j))
-
         def over_x(d):
             local_wait(part_in.at[t, d], rx_r.at[t, d])
             total = part[t, col * SIDE + zs(d)].astype(F32)
@@ -240,9 +238,16 @@
         def _():
             kept_to_x(t + 1)
 
-        @pl.when((t > 0) & (t < ticks - 2))
-        def _():
-            kept_to_z(t + 2)
+
+        @pl.when(t == ticks - 1)
+        def _():
+            for u in range(ticks):
+                rows_u = pl.ds(u * rows, rows)
+                local_wait(kept_pair.at[:, :, rows_u, :], pk_r.at[u])
+                local_wait(scaled_pair.at[rows_u, :], ps_r.at[u])
+            for c in range(SIDE):
+                dw[c] = pair_gradient(far, 1, c).astype(BF16)
+                remote(dw.at[c], dw_in.at[c], dp_s, dp_r.at[c], (s, far, j))
 
         total = jnp.zeros((rows, own_cols), F32)
         squares = jnp.zeros((rows, own_cols), F32)
@@ -267,11 +272,20 @@
                     (up, r, col * SIDE + zs(d)),
                 )
 
+        @pl.when((t > 0) & (t < ticks - 2))
+        def _():
+            kept_to_z(t + 2)
+
+        @pl.when((t > 0) & (t < ticks - 1))
+        def _():
+            kept_to_pair(t)
+
         @pl.when(t == 0)
         def _():
             row_products_over_x(t)
             kept_to_x(1)
             kept_to_z(2)
+            kept_to_pair(0)
 
         local_wait(half_in.at[t], rz_r.at[t])
         branch = keep0[...]
@@ -304,18 +318,18 @@
     loads[7].wait()
     for c in range(SIDE):
         own_sum[c] = pair_gradient(r, 0, c)
-    local_wait(dw_in, dp_r)
     for c in range(SIDE):
-        summed = own_sum[c] + dw_in[c].astype(F32)
-        velocity = MOMENTUM_RATE * mom[c].astype(F32) + summed
+        local_wait(dw_in.at[c], dp_r.at[c])
+        velocity = MOMENTUM_RATE * mom[c].astype(F32) + (own_sum[c] + dw_in[c].astype(F32))
         w_new[c] = (new[c].astype(F32) - LEARNING_RATE * velocity).astype(BF16)
         m_new[c] = velocity.astype(BF16)
-    more = [
-        pltpu.make_async_copy(w_new, w_out, out_sem.at[2]),
-        pltpu.make_async_copy(m_new, m_out, out_sem.at[3]),
-    ]
-    for copy in more:
-        copy.start()
+        more = [
+            pltpu.make_async_copy(w_new.at[c], w_out.at[c], out_sem.at[2 + 2 * c]),
+            pltpu.make_async_copy(m_new.at[c], m_out.at[c], out_sem.at[3 + 2 * c]),
+        ]
+        for copy in more:
+            copy.start()
+        outs += more
 
     for t in range(ticks):
         local_wait(x.at[0, pl.ds(0, SIDE if t else SIDE - 1)], fz_s.at[t])
@@ -331,7 +345,7 @@
         if t:
             local_wait(grad.at[0], g_s.at[t])
     local_wait(dw, dp_s)
-    for copy in outs + more:
+    for copy in outs:
         copy.wait()
 
 
@@ -405,8 +419,8 @@
         dma((ticks,)), dma((ticks,)),
         dma((ticks,)), dma((ticks,)),
         dma((ticks,)), dma((ticks,)),
-        dma, dma,
-        dma((4,)),
+        dma((SIDE,)), dma,
+        dma((2 + 2 * SIDE,)),
     ]
     any_space = pl.BlockSpec(memory_space=pl.ANY)
     shape = jax.ShapeDtypeStruct

time: 163 us -> 158 us (0.969); the launches traced: 160 us -> 158 us
  Pallas kernels: 159 us -> 157 us
    pallas_call x1, Pallas kernels: 157 us -> 155 us  [body(): pl.pallas_call(kernel, name='window', out_shape=(shape((ticks, *block), B...]
where the time goes in v6:
time: 158 us
  Pallas kernels  157 us (99%)
    pallas_call x1, Pallas kernels, body(): pl.pallas_call(kernel, name='window', out_shape=(shape((ticks, *block), B...  155 us

profile of v6, /device:TPU:1, one launch (start us, length us, event | category | flops | bytes accessed | tf_op | source)
XLA Modules:
  0.0 157.7 jit_solution(3869174950652015602)
XLA Ops:
  0.6 154.8 %window.1 = (bf16[4,64,256]{2,1,0:T(8,128)(2,1)}, bf16[4,64,256]{2,1,0:T(8,128)(2,1)}, bf16[4,256,256]{2,1,0:T(8,128)(2,1)}, bf16[4,256,256]{2,1,0:T(8,128)(2,1)}) custom-call(bf16[16,256,256]{2,1,0:T(8,128)(2,1)} %bitcast.12, bf16[4,256,256]{2,1,0:T(8,128)(2,1)} %bitcast.13, bf16[4,256,256]{2,1,0:T(8,128)(2,1)} %bitcast.14, bf16[64,256]{1,0:T(8,128)(2,1)} %bitcast.18, ...), custom_call_target="tpu_custom_call" | custom-call | tf_op jit(solution)/shard_map/window/pallas_call | solution.py:427
  155.4 2.2 %hand_over.1 = (bf16[4,64,256]{2,1,0:T(8,128)(2,1)}, bf16[4,64,256]{2,1,0:T(8,128)(2,1)}, bf16[4,256,256]{2,1,0:T(8,128)(2,1)}, bf16[4,256,256]{2,1,0:T(8,128)(2,1)}) custom-call(bf16[4,64,256]{2,1,0:T(8,128)(2,1)} %get-tuple-element.12.f_in, bf16[4,64,256]{2,1,0:T(8,128)(2,1)} %get-tuple-element.13.b_in, bf16[4,256,256]{2,1,0:T(8,128)(2,1)} %get-tuple-element.14.w_in, ...), custom_call_target="tpu_custom_call" | custom-call | tf_op jit(solution)/shard_map/hand_over/pallas_call | solution.py:452

commit v7 on v6

--- a/solution.py
+++ b/solution.py
@@ -217,18 +217,13 @@
                 pass_on(d)
         keep0[...] = over_x(0)
 
+        local_wait(x.at[t, 0], fz_r.at[t, 2])
+        pass_on(2)
+
         @pl.when(t == 0)
         def _():
             kept_to_x(0)
             kept_to_z(1)
-
-        local_wait(x.at[t, 0], fz_r.at[t, 2])
-        pass_on(2)
-
-        @pl.when(t == 0)
-        def _():
-            kept_products(0)
-            row_products(0)
 
         @pl.when(t > 0)
         def _():
@@ -282,8 +277,10 @@
 
         @pl.when(t == 0)
         def _():
-            row_products_over_x(t)
+            kept_products(0)
+            row_products(0)
             kept_to_x(1)
+            row_products_over_x(0)
             kept_to_z(2)
             kept_to_pair(0)
 

time: 158 us -> 160 us (1.013)
  Pallas kernels: 157 us -> 159 us
    pallas_call x1, Pallas kernels: 155 us -> 157 us  [body(): pl.pallas_call(kernel, name='window', out_shape=(shape((ticks, *block), B...]
where the time goes in v7:
time: 160 us; the launch traced here: 159 us
  Pallas kernels  159 us (99%)
    pallas_call x1, Pallas kernels, body(): pl.pallas_call(kernel, name='window', out_shape=(shape((ticks, *block), B...  157 us

profile of v7, /device:TPU:1, one launch (start us, length us, event | category | flops | bytes accessed | tf_op | source)
XLA Modules:
  0.0 159.4 jit_solution(2263764368342529061)
XLA Ops:
  0.6 156.6 %window.1 = (bf16[4,64,256]{2,1,0:T(8,128)(2,1)}, bf16[4,64,256]{2,1,0:T(8,128)(2,1)}, bf16[4,256,256]{2,1,0:T(8,128)(2,1)}, bf16[4,256,256]{2,1,0:T(8,128)(2,1)}) custom-call(bf16[16,256,256]{2,1,0:T(8,128)(2,1)} %bitcast.12, bf16[4,256,256]{2,1,0:T(8,128)(2,1)} %bitcast.13, bf16[4,256,256]{2,1,0:T(8,128)(2,1)} %bitcast.14, bf16[64,256]{1,0:T(8,128)(2,1)} %bitcast.18, ...), custom_call_target="tpu_custom_call" | custom-call | tf_op jit(solution)/shard_map/window/pallas_call | solution.py:424
  157.2 2.2 %hand_over.1 = (bf16[4,64,256]{2,1,0:T(8,128)(2,1)}, bf16[4,64,256]{2,1,0:T(8,128)(2,1)}, bf16[4,256,256]{2,1,0:T(8,128)(2,1)}, bf16[4,256,256]{2,1,0:T(8,128)(2,1)}) custom-call(bf16[4,64,256]{2,1,0:T(8,128)(2,1)} %get-tuple-element.12.f_in, bf16[4,64,256]{2,1,0:T(8,128)(2,1)} %get-tuple-element.13.b_in, bf16[4,256,256]{2,1,0:T(8,128)(2,1)} %get-tuple-element.14.w_in, ...), custom_call_target="tpu_custom_call" | custom-call | tf_op jit(solution)/shard_map/hand_over/pallas_call | solution.py:449
